TPU v7x, 8 devices: a whole 2x2x1 slice. The times are simulated.
8 devices in a mesh: tp: 4 (over z, y, x), dp: 2 (over core).
Axes of the slice: x: 2, y: 2, z: 1, core: 2. Of those that a mesh axis runs over, the one named last changes fastest.
Arguments:
- x_in: bfloat16 [128, 3072], P(('dp', 'tp'))
- w_gate: bfloat16 [3072, 8192], P('dp', 'tp')
- w_up: bfloat16 [3072, 8192], P('dp', 'tp')
- w_down: bfloat16 [8192, 3072], P('tp', 'dp')
- grad_y: bfloat16 [128, 3072], P(('dp', 'tp'))
Outputs:
- output 1: bfloat16 [128, 3072], P(('dp', 'tp'))
- output 2: bfloat16 [128, 3072], P(('dp', 'tp'))
- output 3: float32 [3072, 8192], P('dp', 'tp')
- output 4: float32 [3072, 8192], P('dp', 'tp')
- output 5: float32 [8192, 3072], P('tp', 'dp')
All inputs are finite; a program needn't handle non-finite values.
Results may differ from a plain program's by a relative error of at most 0.001.
Values are sent between devices in bfloat16 or wider.
A program may use at most 1 GiB of HBM per device.

v0:
```python
import functools

import jax
import jax.numpy as jnp
from jax import lax
from jax.experimental import pallas as pl
from jax.experimental.pallas import tpu as pltpu
from jax.sharding import PartitionSpec as P

MESH = pl.DeviceIdType.MESH
F32 = jnp.float32
BF16 = jnp.bfloat16

NT = (((1,), (1,)), ((), ()))
TN = (((0,), (0,)), ((), ()))

FC = 512
DC = 512
NY = 3


def _front(x_hbm, wg_hbm, wu_hbm, wd_hbm, gy_hbm,
           y_ref, xc_out, gc_out, h_out, da_out, db_out, p_out,
           x_v, gy_v, wg, wu, wd, xc, gc,
           pa, pb, pg, ra, rb, rg, sd, h, da, db,
           yp, yr, dxp,
           w_sem, o_sem, xs, xrs, gs, grs, es, ers, ys, yrs):
    rows, d_full = x_v.shape
    tok, d_half = xc.shape
    ff = wg.shape[1]
    nf = ff // FC
    nd = d_half // DC
    t = lax.axis_index("tp")
    c = lax.axis_index("dp")
    ty, tx = t // 2, t % 2
    peers = []
    for kt in range(4):
        for kc in range(2):
            px = tx if kt % 2 == 0 else 1 - tx
            py = ty if kt // 2 == 0 else 1 - ty
            pc = c if kc == 0 else 1 - c
            peers.append((py * 2 + px, pc))
    order = (6, 7, 2, 3, 4, 5, 1)

    def dev(k):
        return {"tp": peers[k][0], "dp": peers[k][1]}

    def row_of(k):
        return pl.multiple_of((peers[k][1] * 4 + peers[k][0]) * rows, rows)

    def col_of(k):
        return pl.multiple_of(peers[k][1] * d_half, d_half)

    cx = pltpu.make_async_copy(x_hbm, x_v, w_sem.at[0])
    cg = pltpu.make_async_copy(gy_hbm, gy_v, w_sem.at[1])
    cw = [pltpu.make_async_copy(a, b, w_sem.at[2 + i])
          for i, (a, b) in enumerate(((wg_hbm, wg), (wu_hbm, wu), (wd_hbm, wd)))]
    cx.start()
    cg.start()
    for w in cw:
        w.start()

    barrier = pltpu.get_barrier_semaphore()
    for k in range(1, 8):
        pl.semaphore_signal(barrier, inc=1, device_id=dev(k), device_id_type=MESH)
    pl.semaphore_wait(barrier, 7)

    def remote(src, dst, ssem, rsem, k):
        return pltpu.make_async_remote_copy(src_ref=src, dst_ref=dst, send_sem=ssem, recv_sem=rsem,
                                            device_id=dev(k), device_id_type=MESH)

    def spread(own, cols, ssem, rsem):
        out = []
        for k in order:
            cp = remote(own.at[:, pl.ds(col_of(k), d_half)], cols.at[pl.ds(row_of(0), rows), :],
                        ssem.at[k], rsem.at[k], k)
            cp.start()
            out.append(cp)
        return out

    cx.wait()
    sx = spread(x_v, xc, xs, xrs)
    cg.wait()
    sg = spread(gy_v, gc, gs, grs)
    xc[pl.ds(row_of(0), rows), :] = x_v[:, pl.ds(col_of(0), d_half)]
    gc[pl.ds(row_of(0), rows), :] = gy_v[:, pl.ds(col_of(0), d_half)]

    cw[0].wait()
    cw[1].wait()
    for cp in sx:
        cp.wait_recv()
    outs = [pltpu.make_async_copy(xc, xc_out, o_sem.at[0])]
    outs[0].start()
    ex = []
    for j in range(nf):
        f = slice(j * FC, (j + 1) * FC)
        pa[j] = jnp.dot(xc[...], wg[:, f], preferred_element_type=F32)
        ea = remote(pa.at[j], ra.at[j], es.at[3 * j], ers.at[3 * j], 1)
        ea.start()
        pb[j] = jnp.dot(xc[...], wu[:, f], preferred_element_type=F32)
        eb = remote(pb.at[j], rb.at[j], es.at[3 * j + 1], ers.at[3 * j + 1], 1)
        eb.start()
        ex.append((ea, eb))

    rb_rows = 16

    for j in range(nf):
        f = slice(j * FC, (j + 1) * FC)
        ex[j][0].wait_recv()
        ex[j][1].wait_recv()

        def act(i, carry, j=j, f=f):
            r = pl.ds(pl.multiple_of(i * rb_rows, rb_rows), rb_rows)
            a = pa[j, r, :] + ra[j, r, :]
            b = pb[j, r, :] + rb[j, r, :]
            s = jax.nn.sigmoid(a)
            u = a * s
            h[r, f] = (u * b).astype(BF16)
            sd[j, r, :] = s * (1.0 + a * (1.0 - s))
            ra[j, r, :] = u
            rb[j, r, :] = b
            return carry

        lax.fori_loop(0, tok // rb_rows, act, 0)
    outs.append(pltpu.make_async_copy(h, h_out, o_sem.at[1]))
    outs[1].start()

    def reduce_rows(part, recv, n, ssem, rsem):
        out = []
        for k in order:
            cp = remote(part.at[pl.ds(row_of(k), rows), pl.ds(n * DC, DC)],
                        recv.at[k, :, pl.ds(n * DC, DC)],
                        ssem.at[k * nd + n], rsem.at[k * nd + n], k)
            cp.start()
            out.append(cp)
        return out

    cw[2].wait()
    sy = []
    for n in range(nd):
        yp[:, n * DC:(n + 1) * DC] = jnp.dot(h[...], wd[:, n * DC:(n + 1) * DC], preferred_element_type=F32)
        if n < NY:
            sy += reduce_rows(yp, yr, n, ys, yrs)

    for cp in sg:
        cp.wait_recv()
    outs.append(pltpu.make_async_copy(gc, gc_out, o_sem.at[2]))
    outs[2].start()
    eg = []
    for j in range(nf):
        pg[j] = lax.dot_general(gc[...], wd[j * FC:(j + 1) * FC, :], NT, preferred_element_type=F32)
        e = remote(pg.at[j], rg.at[j], es.at[3 * j + 2], ers.at[3 * j + 2], 1)
        e.start()
        eg.append(e)
    for j in range(nf):
        f = slice(j * FC, (j + 1) * FC)
        eg[j].wait_recv()

        def grad(i, carry, j=j, f=f):
            r = pl.ds(pl.multiple_of(i * rb_rows, rb_rows), rb_rows)
            g = pg[j, r, :] + rg[j, r, :]
            da[r, f] = (g * rb[j, r, :] * sd[j, r, :]).astype(BF16)
            db[r, f] = (g * ra[j, r, :]).astype(BF16)
            return carry

        lax.fori_loop(0, tok // rb_rows, grad, 0)
    outs.append(pltpu.make_async_copy(da, da_out, o_sem.at[3]))
    outs.append(pltpu.make_async_copy(db, db_out, o_sem.at[4]))
    outs[3].start()
    outs[4].start()

    for n in range(nd):
        dxp[:, n * DC:(n + 1) * DC] = (
            lax.dot_general(da[...], wg[n * DC:(n + 1) * DC, :], NT, preferred_element_type=F32)
            + lax.dot_general(db[...], wu[n * DC:(n + 1) * DC, :], NT, preferred_element_type=F32))
    for i in range(8):
        r = ((i % 2) * 4 + i // 2) * rows
        p_out[i, :, :d_half] = dxp[r:r + rows, :]
        if NY < nd:
            p_out[i, :, d_half:] = yp[r:r + rows, NY * DC:]

    for cp in sy:
        cp.wait_recv()
    wy = NY * DC
    for kc in range(2 if NY else 0):
        cols = pl.ds(col_of(kc), wy)
        if kc == 0:
            tot = yp[pl.ds(row_of(0), rows), :wy] + yr[2, :, :wy] + yr[4, :, :wy] + yr[6, :, :wy]
        else:
            tot = yr[1, :, :wy] + yr[3, :, :wy] + yr[5, :, :wy] + yr[7, :, :wy]
        y_ref[:, cols] = (x_v[:, cols].astype(F32) + tot).astype(BF16)

    for cp in sx + sg + sy + eg:
        cp.wait_send()
    for ea, eb in ex:
        ea.wait_send()
        eb.wait_send()
    for o in outs:
        o.wait()


def _finish(x, gy, y_part, p, y_ref, dx_ref):
    d_half = x.shape[1] // 2
    wy = NY * DC
    for q in range(2):
        o = q * d_half
        tot = p[q] + p[q + 2] + p[q + 4] + p[q + 6]
        dx_ref[:, o:o + d_half] = (gy[:, o:o + d_half].astype(F32) + tot[:, :d_half]).astype(BF16)
        if NY:
            y_ref[:, o:o + wy] = y_part[:, o:o + wy]
        if wy < d_half:
            y_ref[:, o + wy:o + d_half] = (x[:, o + wy:o + d_half].astype(F32) + tot[:, d_half:]).astype(BF16)


def _grads(h, da, db, xc, gc, dwd_hbm, dwg_hbm, dwu_hbm, buf_d, buf_g, sem_d, sem_g):
    ff = h.shape[1]
    d_half = xc.shape[1]
    nb_d, tr_d = buf_d.shape[:2]
    nb_g, tr_g = buf_g.shape[:2]

    def run(lhs, rhs, out, buf, sem, n, tr, nb, start, prev_out):
        def step(i, carry):
            slot = lax.rem(i + start, nb)
            r = pl.multiple_of(i * tr, tr)

            def drain():
                pltpu.make_async_copy(buf.at[slot], prev_out.at[pl.ds(0, tr), :], sem.at[slot]).wait()

            if start >= nb:
                drain()
            else:
                pl.when(i + start >= nb)(drain)
            buf[slot] = lax.dot_general(lhs[:, pl.ds(r, tr)], rhs[...], TN, preferred_element_type=F32)
            pltpu.make_async_copy(buf.at[slot], out.at[pl.ds(r, tr), :], sem.at[slot]).start()
            return carry

        lax.fori_loop(0, n, step, 0)

    n_d = ff // tr_d
    n_g = d_half // tr_g
    run(h, gc, dwd_hbm, buf_d, sem_d, n_d, tr_d, nb_d, 0, dwd_hbm)
    run(xc, da, dwg_hbm, buf_g, sem_g, n_g, tr_g, nb_g, 0, dwg_hbm)
    run(xc, db, dwu_hbm, buf_g, sem_g, n_g, tr_g, nb_g, n_g, dwu_hbm)
    for s in range(nb_d):
        pltpu.make_async_copy(buf_d.at[s], dwd_hbm.at[pl.ds(0, tr_d), :], sem_d.at[s]).wait()
    for s in range(nb_g):
        pltpu.make_async_copy(buf_g.at[s], dwu_hbm.at[pl.ds(0, tr_g), :], sem_g.at[s]).wait()


def solution(mesh):
    def local_step(x, wg, wu, wd, gy):
        rows, d_full = x.shape
        d_half, ff = wg.shape
        tok = rows * 8
        nf = ff // FC
        nd = d_half // DC
        any_ = pl.BlockSpec(memory_space=pl.ANY)
        hbm = pl.BlockSpec(memory_space=pltpu.HBM)
        vm = pl.BlockSpec(memory_space=pltpu.VMEM)
        S = jax.ShapeDtypeStruct
        dma = pltpu.SemaphoreType.DMA
        part = pltpu.VMEM((nf, tok, FC), F32)
        y, xc, gc, h, da, db, parts = pl.pallas_call(
            _front,
            name="front",
            out_shape=(S((rows, d_full), BF16),
                       S((tok, d_half), BF16), S((tok, d_half), BF16),
                       S((tok, ff), BF16), S((tok, ff), BF16), S((tok, ff), BF16))
            + (S((8, rows, 2 * d_half - NY * DC), F32),),
            in_specs=[hbm] * 5,
            out_specs=(vm,) + (any_,) * 5 + (vm,),
            scratch_shapes=[
                pltpu.VMEM((rows, d_full), BF16), pltpu.VMEM((rows, d_full), BF16),
                pltpu.VMEM((d_half, ff), BF16), pltpu.VMEM((d_half, ff), BF16), pltpu.VMEM((ff, d_half), BF16),
                pltpu.VMEM((tok, d_half), BF16), pltpu.VMEM((tok, d_half), BF16),
                part, part, part, part, part, part, part,
                pltpu.VMEM((tok, ff), BF16), pltpu.VMEM((tok, ff), BF16), pltpu.VMEM((tok, ff), BF16),
                pltpu.VMEM((tok, d_half), F32), pltpu.VMEM((8, rows, d_half), F32),
                pltpu.VMEM((tok, d_half), F32),
                dma((5,)), dma((5,)), dma((8,)), dma((8,)), dma((8,)), dma((8,)),
                dma((3 * nf,)), dma((3 * nf,)),
                dma((8 * nd,)), dma((8 * nd,)),
            ],
            compiler_params=pltpu.CompilerParams(collective_id=0, has_side_effects=True,
                                                 vmem_limit_bytes=50 * 1024 * 1024),
        )(pltpu.with_memory_space_constraint(x, pltpu.HBM), wg, wu, wd,
          pltpu.with_memory_space_constraint(gy, pltpu.HBM))
        parts = lax.all_to_all(parts, ("tp", "dp"), 0, 0, tiled=True)

        tr = 256
        dwd, dwg, dwu = pl.pallas_call(
            _grads,
            name="grads",
            out_shape=(S((ff, d_half), F32), S((d_half, ff), F32), S((d_half, ff), F32)),
            in_specs=[vm] * 5,
            out_specs=(any_, any_, any_),
            scratch_shapes=[pltpu.VMEM((8, tr, d_half), F32), pltpu.VMEM((6, tr, ff), F32),
                            dma((8,)), dma((6,))],
            cost_estimate=pl.CostEstimate(flops=6 * tok * d_half * ff, bytes_accessed=12 * d_half * ff,
                                          transcendentals=0),
            compiler_params=pltpu.CompilerParams(vmem_limit_bytes=50 * 1024 * 1024),
        )(h, da, db, xc, gc)
        y, dx = pl.pallas_call(
            _finish,
            name="finish",
            out_shape=(S((rows, d_full), BF16), S((rows, d_full), BF16)),
            in_specs=[vm] * 4,
            out_specs=(vm, vm),
            compiler_params=pltpu.CompilerParams(vmem_limit_bytes=6 * 1024 * 1024),
        )(x, gy, y, parts)
        return y, dx, dwg, dwu, dwd

    row_spec = P(("dp", "tp"), None)
    up_spec = P("dp", "tp")
    down_spec = P("tp", "dp")
    return jax.shard_map(local_step, mesh=mesh,
                         in_specs=(row_spec, up_spec, up_spec, down_spec, row_spec),
                         out_specs=(row_spec, row_spec, up_spec, up_spec, down_spec),
                         check_vma=False)
```

profile of v0, /device:TPU:0, one launch (start us, length us, event | category | flops | bytes accessed | tf_op | source)
XLA Modules:
  0.0 44.6 jit_solution(17089823919839368211)
XLA Ops:
  0.6 0.0 copy-start.1
  0.6 0.0 copy-start
  0.7 28.1 %front.1 = (bf16[16,3072]{1,0:T(8,128)(2,1)S(1)}, bf16[128,1536]{1,0:T(8,128)(2,1)S(1)}, bf16[128,1536]{1,0:T(8,128)(2,1)S(1)}, bf16[128,2048]{1,0:T(8,128)(2,1)...) custom-call(bf16[16,3072]{1,0:T(8,128)(2,1)} %x.1, ...), custom_call_target="tpu_custom_call" | custom-call | tf_op jit(solution)/shard_map/front/pallas_call | solution.py:263
  28.8 2.3 %all-to-all-start = ((f32[8,16,1536]{2,1,0:T(8,128)}), f32[8,16,1536]{2,1,0:T(8,128)S(1)}, u32[]{:S(2)}, u32[]{:S(2)}) async-start(f32[8,16,1536]{2,1,0:T(8,128)} %get-tuple-element.18), calls=%async_computation | async-start | bytes 1572864 | tf_op jit(solution)/shard_map/all_to_all | solution.py:288
  31.1 12.7 %grads.1 = (f32[2048,1536]{1,0:T(8,128)}, f32[1536,2048]{1,0:T(8,128)}, f32[1536,2048]{1,0:T(8,128)}) custom-call(bf16[128,2048]{1,0:T(8,128)(2,1)S(1)} %get-tuple-element.21.h, bf16[128,2048]{1,0:T(8,128)(2,1)S(1)} %get-tuple-element.22.da, bf16[128,2048]{1,0:T(8,128)(2,1)S(1)} %get-tuple-element.23.db, bf16[128,1536]{1,0:T(8,128)(2,1)S(1)} %get-tuple-element.24.xc, ...), custom_call_target="tpu_custom_call" | custom-call | flops 2415919104 | bytes 37748736 | tf_op jit(solution)/shard_map/grads/pallas_call | solution.py:291
  43.8 0.0 all-to-all-done.p
  43.8 0.0 copy-done.1
  43.8 0.0 copy-done
  43.8 0.7 %finish.1 = (bf16[16,3072]{1,0:T(8,128)(2,1)}, bf16[16,3072]{1,0:T(8,128)(2,1)}) custom-call(bf16[16,3072]{1,0:T(8,128)(2,1)S(1)} %copy-done, bf16[16,3072]{1,0:T(8,128)(2,1)S(1)} %copy-done.1, bf16[16,3072]{1,0:T(8,128)(2,1)S(1)} %get-tuple-element.17.y_part, f32[8,16,1536]{2,1,0:T(8,128)S(1)} %all-to-all-done.p), custom_call_target="tpu_custom_call" | custom-call | tf_op jit(solution)/shard_map/finish/pallas_call | solution.py:303
Async XLA Ops:
  0.6 43.2 %copy-start.1 = (bf16[16,3072]{1,0:T(8,128)(2,1)S(1)}, bf16[16,3072]{1,0:T(8,128)(2,1)}, u32[]{:S(2)}) copy-start(bf16[16,3072]{1,0:T(8,128)(2,1)} %gy.1) | copy-start | bytes 294916
  0.6 43.2 %copy-start = (bf16[16,3072]{1,0:T(8,128)(2,1)S(1)}, bf16[16,3072]{1,0:T(8,128)(2,1)}, u32[]{:S(2)}) copy-start(bf16[16,3072]{1,0:T(8,128)(2,1)} %x.1) | copy-start | bytes 294916
  28.8 15.0 %all-to-all-start = ((f32[8,16,1536]{2,1,0:T(8,128)}), f32[8,16,1536]{2,1,0:T(8,128)S(1)}, u32[]{:S(2)}, u32[]{:S(2)}) async-start(f32[8,16,1536]{2,1,0:T(8,128)} %get-tuple-element.18), calls=%async_computation | async-start | bytes 1572864 | tf_op jit(solution)/shard_map/all_to_all | solution.py:288
where the time goes:
time: 44.7 us; the launch traced here: 44.6 us
  Pallas kernels  41.6 us (93%)
  starting transfers between devices  2.3 us (5%)
  between operations  0.7 us (2%)
    pallas_call x1, Pallas kernels, local_step(): pl.pallas_call(_front, name='front', out_shape=(S((rows, d_full), BF16),...  28.1 us
    pallas_call x1, Pallas kernels, local_step(): pl.pallas_call(_grads, name='grads', out_shape=(S((ff, d_half), F32), S((...  12.7 us
    all_to_all x1, starting transfers between devices, local_step(): parts = lax.all_to_all(parts, ('tp', 'dp'), 0, 0, tiled=True)  2.3 us
  transfers between devices with their start and end apart: 1, of which 0 were waited for; matrix products, arithmetic and copies ran while one was open for 0% of the time, Pallas kernels for 28%

commit v1 on v0

--- a/solution.py
+++ b/solution.py
@@ -16,7 +16,7 @@
 
 FC = 512
 DC = 512
-NY = 3
+NY = 1
 
 
 def _front(x_hbm, wg_hbm, wu_hbm, wd_hbm, gy_hbm,

time: 44.7 us -> 51 us (1.14)
  local copies, waits for them, and re-layouts: 0.01 us -> 3.48 us
  waiting for transfers between devices: 0.01 us -> 3.41 us
  Pallas kernels: 41.6 us -> 40.7 us
    unnamed x4 -> x12, local copies, waits for them, and re-layouts: 0.01 us -> 3.48 us
    all_to_all x1, waiting for transfers between devices: 0.01 us -> 3.41 us  [local_step(): parts = lax.all_to_all(parts, ('tp', 'dp'), 0, 0, tiled=True)]
    pallas_call x1, Pallas kernels: 28.1 us -> 27.3 us  [local_step(): pl.pallas_call(_front, name='front', out_shape=(S((rows, d_full), BF16),...]
  transfers between devices with their start and end apart: 1 -> 1, of which waited for: 0 -> 1; matrix products, arithmetic and copies ran while one was open for 0% -> 0% of each run, Pallas kernels for 28% -> 25%
where the time goes in v1:
time: 51 us; the launch traced here: 50.7 us
  Pallas kernels  40.7 us (80%)
  local copies, waits for them, and re-layouts  3.48 us (7%)
  waiting for transfers between devices  3.41 us (7%)
  starting transfers between devices  2.43 us (5%)
  between operations  0.68 us (1%)
    pallas_call x1, Pallas kernels, local_step(): pl.pallas_call(_front, name='front', out_shape=(S((rows, d_full), BF16),...  27.3 us
    pallas_call x1, Pallas kernels, local_step(): pl.pallas_call(_grads, name='grads', out_shape=(S((ff, d_half), F32), S((...  12.7 us
    unnamed x12, local copies, waits for them, and re-layouts  3.48 us
    all_to_all x1, waiting for transfers between devices, local_step(): parts = lax.all_to_all(parts, ('tp', 'dp'), 0, 0, tiled=True)  3.41 us
    all_to_all x1, starting transfers between devices, local_step(): parts = lax.all_to_all(parts, ('tp', 'dp'), 0, 0, tiled=True)  2.43 us
  transfers between devices with their start and end apart: 1, of which 1 were waited for; matrix products, arithmetic and copies ran while one was open for 0% of the time, Pallas kernels for 25%

profile of v1, /device:TPU:0, one launch (start us, length us, event | category | flops | bytes accessed | tf_op | source)
XLA Modules:
  0.0 50.7 jit_solution(3439193620106063451)
XLA Ops:
  0.6 27.3 %front.1 = (bf16[16,3072]{1,0:T(8,128)(2,1)S(1)}, bf16[128,1536]{1,0:T(8,128)(2,1)S(1)}, bf16[128,1536]{1,0:T(8,128)(2,1)S(1)}, bf16[128,2048]{1,0:T(8,128)(2,1)...) custom-call(bf16[16,3072]{1,0:T(8,128)(2,1)} %x.1, ...), custom_call_target="tpu_custom_call" | custom-call | tf_op jit(solution)/shard_map/front/pallas_call | solution.py:263
  27.9 0.0 copy-start.2
  28.0 0.7 %copy-done.2 = bf16[128,1536]{1,0:T(8,128)(2,1)} copy-done((bf16[128,1536]{1,0:T(8,128)(2,1)}, bf16[128,1536]{1,0:T(8,128)(2,1)S(1)}, u32[]{:S(2)}) %copy-start.2) | copy-done | bytes 393240
  28.7 0.0 copy-start.4
  28.7 0.7 %copy-done.4 = bf16[128,1536]{1,0:T(8,128)(2,1)} copy-done((bf16[128,1536]{1,0:T(8,128)(2,1)}, bf16[128,1536]{1,0:T(8,128)(2,1)S(1)}, u32[]{:S(2)}) %copy-start.4) | copy-done | bytes 393240
  29.4 0.0 copy-start
  29.4 0.0 copy-start.1
  29.4 2.4 %all-to-all-start = ((f32[8,16,2560]{2,1,0:T(8,128)}), f32[8,16,2560]{2,1,0:T(8,128)S(1)}, u32[]{:S(2)}, u32[]{:S(2)}) async-start(f32[8,16,2560]{2,1,0:T(8,128)} %get-tuple-element.18), calls=%async_computation | async-start | bytes 2621440 | tf_op jit(solution)/shard_map/all_to_all | solution.py:288
  31.9 0.0 copy-start.3
  31.9 1.0 %copy-done.3 = bf16[128,1536]{1,0:T(8,128)(2,1)S(1)} copy-done((bf16[128,1536]{1,0:T(8,128)(2,1)S(1)}, bf16[128,1536]{1,0:T(8,128)(2,1)}, u32[]{:S(2)}) %copy-start.3) | copy-done | bytes 393240
  32.9 0.0 copy-start.5
  32.9 1.0 %copy-done.5 = bf16[128,1536]{1,0:T(8,128)(2,1)S(1)} copy-done((bf16[128,1536]{1,0:T(8,128)(2,1)S(1)}, bf16[128,1536]{1,0:T(8,128)(2,1)}, u32[]{:S(2)}) %copy-start.5) | copy-done | bytes 393240
  33.9 12.7 %grads.1 = (f32[2048,1536]{1,0:T(8,128)}, f32[1536,2048]{1,0:T(8,128)}, f32[1536,2048]{1,0:T(8,128)}) custom-call(bf16[128,2048]{1,0:T(8,128)(2,1)S(1)} %get-tuple-element.21.h, bf16[128,2048]{1,0:T(8,128)(2,1)S(1)} %get-tuple-element.22.da, bf16[128,2048]{1,0:T(8,128)(2,1)S(1)} %get-tuple-element.23.db, bf16[128,1536]{1,0:T(8,128)(2,1)S(1)} %copy-done.3, ...), custom_call_target="tpu_custom_call" | custom-call | flops 2415919104 | bytes 37748736 | tf_op jit(solution)/shard_map/grads/pallas_call | solution.py:291
  46.6 3.4 %all-to-all-done.p = f32[8,16,2560]{2,1,0:T(8,128)S(1)} async-done(((f32[8,16,2560]{2,1,0:T(8,128)}), f32[8,16,2560]{2,1,0:T(8,128)S(1)}, u32[]{:S(2)}, u32[]{:S(2)}) %all-to-all-start) | async-done | bytes 1310752 | tf_op jit(solution)/shard_map/all_to_all | solution.py:288
  50.0 0.0 copy-done
  50.0 0.0 copy-done.1
  50.0 0.7 %finish.1 = (bf16[16,3072]{1,0:T(8,128)(2,1)}, bf16[16,3072]{1,0:T(8,128)(2,1)}) custom-call(bf16[16,3072]{1,0:T(8,128)(2,1)S(1)} %copy-done, bf16[16,3072]{1,0:T(8,128)(2,1)S(1)} %copy-done.1, bf16[16,3072]{1,0:T(8,128)(2,1)S(1)} %get-tuple-element.17.y_part, f32[8,16,2560]{2,1,0:T(8,128)S(1)} %all-to-all-done.p), custom_call_target="tpu_custom_call" | custom-call | tf_op jit(solution)/shard_map/finish/pallas_call | solution.py:303
Async XLA Ops:
  27.9 0.7 %copy-start.2 = (bf16[128,1536]{1,0:T(8,128)(2,1)}, bf16[128,1536]{1,0:T(8,128)(2,1)S(1)}, u32[]{:S(2)}) copy-start(bf16[128,1536]{1,0:T(8,128)(2,1)S(1)} %get-tuple-element.24.xc) | copy-start | bytes 1179652
  28.7 0.7 %copy-start.4 = (bf16[128,1536]{1,0:T(8,128)(2,1)}, bf16[128,1536]{1,0:T(8,128)(2,1)S(1)}, u32[]{:S(2)}) copy-start(bf16[128,1536]{1,0:T(8,128)(2,1)S(1)} %get-tuple-element.25.gc) | copy-start | bytes 1179652
  29.4 20.5 %copy-start = (bf16[16,3072]{1,0:T(8,128)(2,1)S(1)}, bf16[16,3072]{1,0:T(8,128)(2,1)}, u32[]{:S(2)}) copy-start(bf16[16,3072]{1,0:T(8,128)(2,1)} %x.1) | copy-start | bytes 294916
  29.4 20.5 %copy-start.1 = (bf16[16,3072]{1,0:T(8,128)(2,1)S(1)}, bf16[16,3072]{1,0:T(8,128)(2,1)}, u32[]{:S(2)}) copy-start(bf16[16,3072]{1,0:T(8,128)(2,1)} %gy.1) | copy-start | bytes 294916
  29.4 20.5 %all-to-all-start = ((f32[8,16,2560]{2,1,0:T(8,128)}), f32[8,16,2560]{2,1,0:T(8,128)S(1)}, u32[]{:S(2)}, u32[]{:S(2)}) async-start(f32[8,16,2560]{2,1,0:T(8,128)} %get-tuple-element.18), calls=%async_computation | async-start | bytes 2621440 | tf_op jit(solution)/shard_map/all_to_all | solution.py:288
  31.9 1.0 %copy-start.3 = (bf16[128,1536]{1,0:T(8,128)(2,1)S(1)}, bf16[128,1536]{1,0:T(8,128)(2,1)}, u32[]{:S(2)}) copy-start(bf16[128,1536]{1,0:T(8,128)(2,1)} %copy-done.2) | copy-start | bytes 1179652
  32.9 1.0 %copy-start.5 = (bf16[128,1536]{1,0:T(8,128)(2,1)S(1)}, bf16[128,1536]{1,0:T(8,128)(2,1)}, u32[]{:S(2)}) copy-start(bf16[128,1536]{1,0:T(8,128)(2,1)} %copy-done.4) | copy-start | bytes 1179652

commit v2 on v0

--- a/solution.py
+++ b/solution.py
@@ -57,8 +57,6 @@
           for i, (a, b) in enumerate(((wg_hbm, wg), (wu_hbm, wu), (wd_hbm, wd)))]
     cx.start()
     cg.start()
-    for w in cw:
-        w.start()
 
     barrier = pltpu.get_barrier_semaphore()
     for k in range(1, 8):
@@ -82,6 +80,8 @@
     sx = spread(x_v, xc, xs, xrs)
     cg.wait()
     sg = spread(gy_v, gc, gs, grs)
+    for w in cw:
+        w.start()
     xc[pl.ds(row_of(0), rows), :] = x_v[:, pl.ds(col_of(0), d_half)]
     gc[pl.ds(row_of(0), rows), :] = gy_v[:, pl.ds(col_of(0), d_half)]
 

time: 44.7 us -> 44.7 us (level)
  no operation moved by 1% of the time
where the time goes in v2:
time: 44.7 us; the launch traced here: 44.6 us
  Pallas kernels  41.6 us (93%)
  starting transfers between devices  2.3 us (5%)
  between operations  0.7 us (2%)
    pallas_call x1, Pallas kernels, local_step(): pl.pallas_call(_front, name='front', out_shape=(S((rows, d_full), BF16),...  28.1 us
    pallas_call x1, Pallas kernels, local_step(): pl.pallas_call(_grads, name='grads', out_shape=(S((ff, d_half), F32), S((...  12.7 us
    all_to_all x1, starting transfers between devices, local_step(): parts = lax.all_to_all(parts, ('tp', 'dp'), 0, 0, tiled=True)  2.3 us
  transfers between devices with their start and end apart: 1, of which 0 were waited for; matrix products, arithmetic and copies ran while one was open for 0% of the time, Pallas kernels for 28%

profile of v2, /device:TPU:0, one launch (start us, length us, event | category | flops | bytes accessed | tf_op | source)
XLA Modules:
  0.0 44.6 jit_solution(7838514770534857875)
XLA Ops:
  0.6 0.0 copy-start.1
  0.6 0.0 copy-start
  0.7 28.1 %front.1 = (bf16[16,3072]{1,0:T(8,128)(2,1)S(1)}, bf16[128,1536]{1,0:T(8,128)(2,1)S(1)}, bf16[128,1536]{1,0:T(8,128)(2,1)S(1)}, bf16[128,2048]{1,0:T(8,128)(2,1)...) custom-call(bf16[16,3072]{1,0:T(8,128)(2,1)} %x.1, ...), custom_call_target="tpu_custom_call" | custom-call | tf_op jit(solution)/shard_map/front/pallas_call | solution.py:263
  28.8 2.3 %all-to-all-start = ((f32[8,16,1536]{2,1,0:T(8,128)}), f32[8,16,1536]{2,1,0:T(8,128)S(1)}, u32[]{:S(2)}, u32[]{:S(2)}) async-start(f32[8,16,1536]{2,1,0:T(8,128)} %get-tuple-element.18), calls=%async_computation | async-start | bytes 1572864 | tf_op jit(solution)/shard_map/all_to_all | solution.py:288
  31.1 12.7 %grads.1 = (f32[2048,1536]{1,0:T(8,128)}, f32[1536,2048]{1,0:T(8,128)}, f32[1536,2048]{1,0:T(8,128)}) custom-call(bf16[128,2048]{1,0:T(8,128)(2,1)S(1)} %get-tuple-element.21.h, bf16[128,2048]{1,0:T(8,128)(2,1)S(1)} %get-tuple-element.22.da, bf16[128,2048]{1,0:T(8,128)(2,1)S(1)} %get-tuple-element.23.db, bf16[128,1536]{1,0:T(8,128)(2,1)S(1)} %get-tuple-element.24.xc, ...), custom_call_target="tpu_custom_call" | custom-call | flops 2415919104 | bytes 37748736 | tf_op jit(solution)/shard_map/grads/pallas_call | solution.py:291
  43.8 0.0 all-to-all-done.p
  43.8 0.0 copy-done.1
  43.8 0.0 copy-done
  43.8 0.7 %finish.1 = (bf16[16,3072]{1,0:T(8,128)(2,1)}, bf16[16,3072]{1,0:T(8,128)(2,1)}) custom-call(bf16[16,3072]{1,0:T(8,128)(2,1)S(1)} %copy-done, bf16[16,3072]{1,0:T(8,128)(2,1)S(1)} %copy-done.1, bf16[16,3072]{1,0:T(8,128)(2,1)S(1)} %get-tuple-element.17.y_part, f32[8,16,1536]{2,1,0:T(8,128)S(1)} %all-to-all-done.p), custom_call_target="tpu_custom_call" | custom-call | tf_op jit(solution)/shard_map/finish/pallas_call | solution.py:303
Async XLA Ops:
  0.6 43.2 %copy-start.1 = (bf16[16,3072]{1,0:T(8,128)(2,1)S(1)}, bf16[16,3072]{1,0:T(8,128)(2,1)}, u32[]{:S(2)}) copy-start(bf16[16,3072]{1,0:T(8,128)(2,1)} %gy.1) | copy-start | bytes 294916
  0.6 43.2 %copy-start = (bf16[16,3072]{1,0:T(8,128)(2,1)S(1)}, bf16[16,3072]{1,0:T(8,128)(2,1)}, u32[]{:S(2)}) copy-start(bf16[16,3072]{1,0:T(8,128)(2,1)} %x.1) | copy-start | bytes 294916
  28.8 15.0 %all-to-all-start = ((f32[8,16,1536]{2,1,0:T(8,128)}), f32[8,16,1536]{2,1,0:T(8,128)S(1)}, u32[]{:S(2)}, u32[]{:S(2)}) async-start(f32[8,16,1536]{2,1,0:T(8,128)} %get-tuple-element.18), calls=%async_computation | async-start | bytes 1572864 | tf_op jit(solution)/shard_map/all_to_all | solution.py:288

commit v3 on v1

--- a/solution.py
+++ b/solution.py
@@ -16,7 +16,7 @@
 
 FC = 512
 DC = 512
-NY = 1
+NY = 2
 
 
 def _front(x_hbm, wg_hbm, wu_hbm, wd_hbm, gy_hbm,
@@ -80,9 +80,11 @@
 
     cx.wait()
     sx = spread(x_v, xc, xs, xrs)
+    xc[pl.ds(row_of(0), rows), :] = x_v[:, pl.ds(col_of(0), d_half)]
     cg.wait()
+    for cp in sx:
+        cp.wait_send()
     sg = spread(gy_v, gc, gs, grs)
-    xc[pl.ds(row_of(0), rows), :] = x_v[:, pl.ds(col_of(0), d_half)]
     gc[pl.ds(row_of(0), rows), :] = gy_v[:, pl.ds(col_of(0), d_half)]
 
     cw[0].wait()
@@ -164,15 +166,15 @@
             return carry
 
         lax.fori_loop(0, tok // rb_rows, grad, 0)
+        for n in range(nd):
+            o = slice(n * DC, (n + 1) * DC)
+            part = (lax.dot_general(da[:, f], wg[o, f], NT, preferred_element_type=F32)
+                    + lax.dot_general(db[:, f], wu[o, f], NT, preferred_element_type=F32))
+            dxp[:, o] = part if j == 0 else dxp[:, o] + part
     outs.append(pltpu.make_async_copy(da, da_out, o_sem.at[3]))
     outs.append(pltpu.make_async_copy(db, db_out, o_sem.at[4]))
     outs[3].start()
     outs[4].start()
-
-    for n in range(nd):
-        dxp[:, n * DC:(n + 1) * DC] = (
-            lax.dot_general(da[...], wg[n * DC:(n + 1) * DC, :], NT, preferred_element_type=F32)
-            + lax.dot_general(db[...], wu[n * DC:(n + 1) * DC, :], NT, preferred_element_type=F32))
     for i in range(8):
         r = ((i % 2) * 4 + i // 2) * rows
         p_out[i, :, :d_half] = dxp[r:r + rows, :]
@@ -190,7 +192,7 @@
             tot = yr[1, :, :wy] + yr[3, :, :wy] + yr[5, :, :wy] + yr[7, :, :wy]
         y_ref[:, cols] = (x_v[:, cols].astype(F32) + tot).astype(BF16)
 
-    for cp in sx + sg + sy + eg:
+    for cp in sg + sy + eg:
         cp.wait_send()
     for ea, eb in ex:
         ea.wait_send()
@@ -282,7 +284,7 @@
                 dma((8 * nd,)), dma((8 * nd,)),
             ],
             compiler_params=pltpu.CompilerParams(collective_id=0, has_side_effects=True,
-                                                 vmem_limit_bytes=50 * 1024 * 1024),
+                                                 vmem_limit_bytes=40 * 1024 * 1024),
         )(pltpu.with_memory_space_constraint(x, pltpu.HBM), wg, wu, wd,
           pltpu.with_memory_space_constraint(gy, pltpu.HBM))
         parts = lax.all_to_all(parts, ("tp", "dp"), 0, 0, tiled=True)
@@ -298,7 +300,7 @@
                             dma((8,)), dma((6,))],
             cost_estimate=pl.CostEstimate(flops=6 * tok * d_half * ff, bytes_accessed=12 * d_half * ff,
                                           transcendentals=0),
-            compiler_params=pltpu.CompilerParams(vmem_limit_bytes=50 * 1024 * 1024),
+            compiler_params=pltpu.CompilerParams(vmem_limit_bytes=34 * 1024 * 1024),
         )(h, da, db, xc, gc)
         y, dx = pl.pallas_call(
             _finish,

time: 51 us -> 48.7 us (0.955)
  waiting for transfers between devices: 3.41 us -> 1.59 us
  Pallas kernels: 40.7 us -> 39.4 us
  local copies, waits for them, and re-layouts: 3.48 us -> 4.52 us
    all_to_all x1, waiting for transfers between devices: 3.41 us -> 1.59 us  [local_step(): parts = lax.all_to_all(parts, ('tp', 'dp'), 0, 0, tiled=True)]
    pallas_call x1, Pallas kernels: 27.3 us -> 26 us  [local_step(): pl.pallas_call(_front, name='front', out_shape=(S((rows, d_full), BF16),...]
    unnamed x12 -> x10, local copies, waits for them, and re-layouts: 3.48 us -> 4.52 us
  transfers between devices with their start and end apart: 1 -> 1, of which waited for: 1 -> 1; matrix products, arithmetic and copies ran while one was open for 0% -> 0% of each run, Pallas kernels for 25% -> 26%
where the time goes in v3:
time: 48.7 us; the launch traced here: 48.5 us
  Pallas kernels  39.4 us (81%)
  local copies, waits for them, and re-layouts  4.52 us (9%)
  starting transfers between devices  2.29 us (5%)
  waiting for transfers between devices  1.59 us (3%)
  between operations  0.68 us (1%)
    pallas_call x1, Pallas kernels, local_step(): pl.pallas_call(_front, name='front', out_shape=(S((rows, d_full), BF16),...  26 us
    pallas_call x1, Pallas kernels, local_step(): pl.pallas_call(_grads, name='grads', out_shape=(S((ff, d_half), F32), S((...  12.7 us
    unnamed x10, local copies, waits for them, and re-layouts  4.52 us
    all_to_all x1, starting transfers between devices, local_step(): parts = lax.all_to_all(parts, ('tp', 'dp'), 0, 0, tiled=True)  2.29 us
    all_to_all x1, waiting for transfers between devices, local_step(): parts = lax.all_to_all(parts, ('tp', 'dp'), 0, 0, tiled=True)  1.59 us
  transfers between devices with their start and end apart: 1, of which 1 were waited for; matrix products, arithmetic and copies ran while one was open for 0% of the time, Pallas kernels for 26%

profile of v3, /device:TPU:0, one launch (start us, length us, event | category | flops | bytes accessed | tf_op | source)
XLA Modules:
  0.0 48.5 jit_solution(2611325942770634790)
XLA Ops:
  0.6 0.0 copy-start
  0.6 2.8 %copy-done = bf16[1536,2048]{1,0:T(8,128)(2,1)S(1)} copy-done((bf16[1536,2048]{1,0:T(8,128)(2,1)S(1)}, bf16[1536,2048]{1,0:T(8,128)(2,1)}, u32[]{:S(2)}) %copy-start) | copy-done | bytes 6291480
  3.4 0.0 copy-start.1
  3.4 0.0 copy-start.2
  3.4 26.0 %front.1 = (bf16[16,3072]{1,0:T(8,128)(2,1)S(1)}, bf16[128,1536]{1,0:T(8,128)(2,1)S(1)}, bf16[128,1536]{1,0:T(8,128)(2,1)S(1)}, bf16[128,2048]{1,0:T(8,128)(2,1)...) custom-call(bf16[16,3072]{1,0:T(8,128)(2,1)} %x.1, ...), custom_call_target="tpu_custom_call" | custom-call | tf_op jit(solution)/shard_map/front/pallas_call | solution.py:265
  29.4 0.0 copy-start.3
  29.4 0.7 %copy-done.3 = bf16[128,1536]{1,0:T(8,128)(2,1)} copy-done((bf16[128,1536]{1,0:T(8,128)(2,1)}, bf16[128,1536]{1,0:T(8,128)(2,1)S(1)}, u32[]{:S(2)}) %copy-start.3) | copy-done | bytes 393240
  30.2 2.3 %all-to-all-start = ((f32[8,16,2048]{2,1,0:T(8,128)}), f32[8,16,2048]{2,1,0:T(8,128)S(1)}, u32[]{:S(2)}, u32[]{:S(2)}) async-start(f32[8,16,2048]{2,1,0:T(8,128)} %get-tuple-element.18), calls=%async_computation | async-start | bytes 2097152 | tf_op jit(solution)/shard_map/all_to_all | solution.py:290
  32.5 0.0 copy-start.4
  32.5 1.0 %copy-done.4 = bf16[128,1536]{1,0:T(8,128)(2,1)S(1)} copy-done((bf16[128,1536]{1,0:T(8,128)(2,1)S(1)}, bf16[128,1536]{1,0:T(8,128)(2,1)}, u32[]{:S(2)}) %copy-start.4) | copy-done | bytes 393240
  33.5 12.7 %grads.1 = (f32[2048,1536]{1,0:T(8,128)}, f32[1536,2048]{1,0:T(8,128)}, f32[1536,2048]{1,0:T(8,128)}) custom-call(bf16[128,2048]{1,0:T(8,128)(2,1)S(1)} %get-tuple-element.21.h, bf16[128,2048]{1,0:T(8,128)(2,1)S(1)} %get-tuple-element.22.da, bf16[128,2048]{1,0:T(8,128)(2,1)S(1)} %get-tuple-element.23.db, bf16[128,1536]{1,0:T(8,128)(2,1)S(1)} %get-tuple-element.24.xc, ...), custom_call_target="tpu_custom_call" | custom-call | flops 2415919104 | bytes 37748736 | tf_op jit(solution)/shard_map/grads/pallas_call | solution.py:293
  46.2 1.6 %all-to-all-done.p = f32[8,16,2048]{2,1,0:T(8,128)S(1)} async-done(((f32[8,16,2048]{2,1,0:T(8,128)}), f32[8,16,2048]{2,1,0:T(8,128)S(1)}, u32[]{:S(2)}, u32[]{:S(2)}) %all-to-all-start) | async-done | bytes 1048608 | tf_op jit(solution)/shard_map/all_to_all | solution.py:290
  47.8 0.0 copy-done.1
  47.8 0.0 copy-done.2
  47.8 0.7 %finish.1 = (bf16[16,3072]{1,0:T(8,128)(2,1)}, bf16[16,3072]{1,0:T(8,128)(2,1)}) custom-call(bf16[16,3072]{1,0:T(8,128)(2,1)S(1)} %copy-done.1, bf16[16,3072]{1,0:T(8,128)(2,1)S(1)} %copy-done.2, bf16[16,3072]{1,0:T(8,128)(2,1)S(1)} %get-tuple-element.17.y_part, f32[8,16,2048]{2,1,0:T(8,128)S(1)} %all-to-all-done.p), custom_call_target="tpu_custom_call" | custom-call | tf_op jit(solution)/shard_map/finish/pallas_call | solution.py:305
Async XLA Ops:
  0.6 2.8 %copy-start = (bf16[1536,2048]{1,0:T(8,128)(2,1)S(1)}, bf16[1536,2048]{1,0:T(8,128)(2,1)}, u32[]{:S(2)}) copy-start(bf16[1536,2048]{1,0:T(8,128)(2,1)} %wg_hbm.1) | copy-start | bytes 18874372
  3.4 44.3 %copy-start.1 = (bf16[16,3072]{1,0:T(8,128)(2,1)S(1)}, bf16[16,3072]{1,0:T(8,128)(2,1)}, u32[]{:S(2)}) copy-start(bf16[16,3072]{1,0:T(8,128)(2,1)} %x.1) | copy-start | bytes 294916
  3.4 44.3 %copy-start.2 = (bf16[16,3072]{1,0:T(8,128)(2,1)S(1)}, bf16[16,3072]{1,0:T(8,128)(2,1)}, u32[]{:S(2)}) copy-start(bf16[16,3072]{1,0:T(8,128)(2,1)} %gy.1) | copy-start | bytes 294916
  29.4 0.7 %copy-start.3 = (bf16[128,1536]{1,0:T(8,128)(2,1)}, bf16[128,1536]{1,0:T(8,128)(2,1)S(1)}, u32[]{:S(2)}) copy-start(bf16[128,1536]{1,0:T(8,128)(2,1)S(1)} %get-tuple-element.25.gc) | copy-start | bytes 1179652
  30.2 17.6 %all-to-all-start = ((f32[8,16,2048]{2,1,0:T(8,128)}), f32[8,16,2048]{2,1,0:T(8,128)S(1)}, u32[]{:S(2)}, u32[]{:S(2)}) async-start(f32[8,16,2048]{2,1,0:T(8,128)} %get-tuple-element.18), calls=%async_computation | async-start | bytes 2097152 | tf_op jit(solution)/shard_map/all_to_all | solution.py:290
  32.5 1.0 %copy-start.4 = (bf16[128,1536]{1,0:T(8,128)(2,1)S(1)}, bf16[128,1536]{1,0:T(8,128)(2,1)}, u32[]{:S(2)}) copy-start(bf16[128,1536]{1,0:T(8,128)(2,1)} %copy-done.3) | copy-start | bytes 1179652

commit v4 on v3

--- a/solution.py
+++ b/solution.py
@@ -180,6 +180,12 @@
         p_out[i, :, :d_half] = dxp[r:r + rows, :]
         if NY < nd:
             p_out[i, :, d_half:] = yp[r:r + rows, NY * DC:]
+    for q in range(2):
+        i = t * 2 + q
+        r = pl.ds(pl.multiple_of((q * 4 + t) * rows, rows), rows)
+        p_out[i, :, :d_half] += gc[r, :].astype(F32)
+        if NY < nd:
+            p_out[i, :, d_half:] += xc[r, NY * DC:].astype(F32)
 
     for cp in sy:
         cp.wait_recv()
@@ -201,24 +207,26 @@
         o.wait()
 
 
-def _finish(x, gy, y_part, p, y_ref, dx_ref):
-    d_half = x.shape[1] // 2
+def _finish(y_part, p, y_ref, dx_ref):
+    d_half = y_ref.shape[1] // 2
     wy = NY * DC
     for q in range(2):
         o = q * d_half
         tot = p[q] + p[q + 2] + p[q + 4] + p[q + 6]
-        dx_ref[:, o:o + d_half] = (gy[:, o:o + d_half].astype(F32) + tot[:, :d_half]).astype(BF16)
+        dx_ref[:, o:o + d_half] = tot[:, :d_half].astype(BF16)
         if NY:
             y_ref[:, o:o + wy] = y_part[:, o:o + wy]
         if wy < d_half:
-            y_ref[:, o + wy:o + d_half] = (x[:, o + wy:o + d_half].astype(F32) + tot[:, d_half:]).astype(BF16)
-
-
-def _grads(h, da, db, xc, gc, dwd_hbm, dwg_hbm, dwu_hbm, buf_d, buf_g, sem_d, sem_g):
+            y_ref[:, o + wy:o + d_half] = tot[:, d_half:].astype(BF16)
+
+
+def _grads(h, da, db, xc_hbm, gc, dwd_hbm, dwg_hbm, dwu_hbm, buf_d, buf_g, xc, sem_d, sem_g, sem_x):
     ff = h.shape[1]
     d_half = xc.shape[1]
     nb_d, tr_d = buf_d.shape[:2]
     nb_g, tr_g = buf_g.shape[:2]
+    cx = pltpu.make_async_copy(xc_hbm, xc, sem_x)
+    cx.start()
 
     def run(lhs, rhs, out, buf, sem, n, tr, nb, start, prev_out):
         def step(i, carry):
@@ -241,6 +249,7 @@
     n_d = ff // tr_d
     n_g = d_half // tr_g
     run(h, gc, dwd_hbm, buf_d, sem_d, n_d, tr_d, nb_d, 0, dwd_hbm)
+    cx.wait()
     run(xc, da, dwg_hbm, buf_g, sem_g, n_g, tr_g, nb_g, 0, dwg_hbm)
     run(xc, db, dwu_hbm, buf_g, sem_g, n_g, tr_g, nb_g, n_g, dwu_hbm)
     for s in range(nb_d):
@@ -266,11 +275,11 @@
             _front,
             name="front",
             out_shape=(S((rows, d_full), BF16),
-                       S((tok, d_half), BF16), S((tok, d_half), BF16),
+                       pltpu.HBM((tok, d_half), BF16), S((tok, d_half), BF16),
                        S((tok, ff), BF16), S((tok, ff), BF16), S((tok, ff), BF16))
             + (S((8, rows, 2 * d_half - NY * DC), F32),),
             in_specs=[hbm] * 5,
-            out_specs=(vm,) + (any_,) * 5 + (vm,),
+            out_specs=(vm, hbm, any_, any_, any_, any_, vm),
             scratch_shapes=[
                 pltpu.VMEM((rows, d_full), BF16), pltpu.VMEM((rows, d_full), BF16),
                 pltpu.VMEM((d_half, ff), BF16), pltpu.VMEM((d_half, ff), BF16), pltpu.VMEM((ff, d_half), BF16),
@@ -284,9 +293,8 @@
                 dma((8 * nd,)), dma((8 * nd,)),
             ],
             compiler_params=pltpu.CompilerParams(collective_id=0, has_side_effects=True,
-                                                 vmem_limit_bytes=40 * 1024 * 1024),
-        )(pltpu.with_memory_space_constraint(x, pltpu.HBM), wg, wu, wd,
-          pltpu.with_memory_space_constraint(gy, pltpu.HBM))
+                                                 vmem_limit_bytes=50 * 1024 * 1024),
+        )(*(pltpu.with_memory_space_constraint(v, pltpu.HBM) for v in (x, wg, wu, wd, gy)))
         parts = lax.all_to_all(parts, ("tp", "dp"), 0, 0, tiled=True)
 
         tr = 256
@@ -294,22 +302,22 @@
             _grads,
             name="grads",
             out_shape=(S((ff, d_half), F32), S((d_half, ff), F32), S((d_half, ff), F32)),
-            in_specs=[vm] * 5,
+            in_specs=[vm, vm, vm, hbm, vm],
             out_specs=(any_, any_, any_),
             scratch_shapes=[pltpu.VMEM((8, tr, d_half), F32), pltpu.VMEM((6, tr, ff), F32),
-                            dma((8,)), dma((6,))],
+                            pltpu.VMEM((tok, d_half), BF16), dma((8,)), dma((6,)), dma(())],
             cost_estimate=pl.CostEstimate(flops=6 * tok * d_half * ff, bytes_accessed=12 * d_half * ff,
                                           transcendentals=0),
             compiler_params=pltpu.CompilerParams(vmem_limit_bytes=34 * 1024 * 1024),
-        )(h, da, db, xc, gc)
+        )(h, da, db, pltpu.with_memory_space_constraint(xc, pltpu.HBM), gc)
         y, dx = pl.pallas_call(
             _finish,
             name="finish",
             out_shape=(S((rows, d_full), BF16), S((rows, d_full), BF16)),
-            in_specs=[vm] * 4,
+            in_specs=[vm] * 2,
             out_specs=(vm, vm),
             compiler_params=pltpu.CompilerParams(vmem_limit_bytes=6 * 1024 * 1024),
-        )(x, gy, y, parts)
+        )(y, parts)
         return y, dx, dwg, dwu, dwd
 
     row_spec = P(("dp", "tp"), None)

time: 48.7 us -> 45.8 us (0.940)
  local copies, waits for them, and re-layouts: 4.52 us -> 0 us
  waiting for transfers between devices: 1.59 us -> 2.58 us
  Pallas kernels: 39.4 us -> 40.1 us
    unnamed x10 -> x0, local copies, waits for them, and re-layouts: 4.52 us -> none
    all_to_all x1, waiting for transfers between devices: 1.59 us -> 2.58 us  [local_step(): parts = lax.all_to_all(parts, ('tp', 'dp'), 0, 0, tiled=True)]
    pallas_call x1, Pallas kernels: 26 us -> 26.7 us  [local_step(): pl.pallas_call(_front, name='front', out_shape=(S((rows, d_full), BF16),...]
  transfers between devices with their start and end apart: 1 -> 1, of which waited for: 1 -> 1; matrix products, arithmetic and copies ran while one was open for 0% -> 0% of each run, Pallas kernels for 26% -> 28%
where the time goes in v4:
time: 45.8 us; the launch traced here: 45.6 us
  Pallas kernels  40.1 us (88%)
  waiting for transfers between devices  2.58 us (6%)
  starting transfers between devices  2.31 us (5%)
  between operations  0.66 us (1%)
    pallas_call x1, Pallas kernels, local_step(): pl.pallas_call(_front, name='front', out_shape=(S((rows, d_full), BF16),...  26.7 us
    pallas_call x1, Pallas kernels, local_step(): pl.pallas_call(_grads, name='grads', out_shape=(S((ff, d_half), F32), S((...  12.7 us
    all_to_all x1, waiting for transfers between devices, local_step(): parts = lax.all_to_all(parts, ('tp', 'dp'), 0, 0, tiled=True)  2.58 us
    all_to_all x1, starting transfers between devices, local_step(): parts = lax.all_to_all(parts, ('tp', 'dp'), 0, 0, tiled=True)  2.31 us
  transfers between devices with their start and end apart: 1, of which 1 were waited for; matrix products, arithmetic and copies ran while one was open for 0% of the time, Pallas kernels for 28%

profile of v4, /device:TPU:0, one launch (start us, length us, event | category | flops | bytes accessed | tf_op | source)
XLA Modules:
  0.0 45.6 jit_solution(9781900776597496796)
XLA Ops:
  0.6 26.7 %front.1 = (bf16[16,3072]{1,0:T(8,128)(2,1)S(1)}, bf16[128,1536]{1,0:T(8,128)(2,1)}, bf16[128,1536]{1,0:T(8,128)(2,1)S(1)}, bf16[128,2048]{1,0:T(8,128)(2,1)S(1)...) custom-call(bf16[16,3072]{1,0:T(8,128)(2,1)} %x_hbm.1, ...), custom_call_target="tpu_custom_call" | custom-call | tf_op jit(solution)/shard_map/front/pallas_call | solution.py:274
  27.3 2.3 %all-to-all-start = ((f32[8,16,2048]{2,1,0:T(8,128)}), f32[8,16,2048]{2,1,0:T(8,128)S(1)}, u32[]{:S(2)}, u32[]{:S(2)}) async-start(f32[8,16,2048]{2,1,0:T(8,128)} %get-tuple-element.18), calls=%async_computation | async-start | bytes 2097152 | tf_op jit(solution)/shard_map/all_to_all | solution.py:298
  29.6 12.7 %grads.1 = (f32[2048,1536]{1,0:T(8,128)}, f32[1536,2048]{1,0:T(8,128)}, f32[1536,2048]{1,0:T(8,128)}) custom-call(bf16[128,2048]{1,0:T(8,128)(2,1)S(1)} %get-tuple-element.21.h, bf16[128,2048]{1,0:T(8,128)(2,1)S(1)} %get-tuple-element.22.da, bf16[128,2048]{1,0:T(8,128)(2,1)S(1)} %get-tuple-element.23.db, bf16[128,1536]{1,0:T(8,128)(2,1)} %get-tuple-element.24.xc_hbm, ...), custom_call_target="tpu_custom_call" | custom-call | flops 2415919104 | bytes 37748736 | tf_op jit(solution)/shard_map/grads/pallas_call | solution.py:301
  42.3 2.6 %all-to-all-done.p = f32[8,16,2048]{2,1,0:T(8,128)S(1)} async-done(((f32[8,16,2048]{2,1,0:T(8,128)}), f32[8,16,2048]{2,1,0:T(8,128)S(1)}, u32[]{:S(2)}, u32[]{:S(2)}) %all-to-all-start) | async-done | bytes 1048608 | tf_op jit(solution)/shard_map/all_to_all | solution.py:298
  44.9 0.7 %finish.1 = (bf16[16,3072]{1,0:T(8,128)(2,1)}, bf16[16,3072]{1,0:T(8,128)(2,1)}) custom-call(bf16[16,3072]{1,0:T(8,128)(2,1)S(1)} %get-tuple-element.17.y_part, f32[8,16,2048]{2,1,0:T(8,128)S(1)} %all-to-all-done.p), custom_call_target="tpu_custom_call" | custom-call | tf_op jit(solution)/shard_map/finish/pallas_call | solution.py:313
Async XLA Ops:
  27.3 17.6 %all-to-all-start = ((f32[8,16,2048]{2,1,0:T(8,128)}), f32[8,16,2048]{2,1,0:T(8,128)S(1)}, u32[]{:S(2)}, u32[]{:S(2)}) async-start(f32[8,16,2048]{2,1,0:T(8,128)} %get-tuple-element.18), calls=%async_computation | async-start | bytes 2097152 | tf_op jit(solution)/shard_map/all_to_all | solution.py:298

commit v5 on v4

v5 whole, which is shorter than its diff:
```python
import functools

import jax
import jax.numpy as jnp
from jax import lax
from jax.experimental import pallas as pl
from jax.experimental.pallas import tpu as pltpu
from jax.sharding import PartitionSpec as P

MESH = pl.DeviceIdType.MESH
F32 = jnp.float32
BF16 = jnp.bfloat16

NT = (((1,), (1,)), ((), ()))
TN = (((0,), (0,)), ((), ()))

FC = 512
DC = 512
RB = 32


def _front(x_hbm, wg_hbm, wu_hbm, wd_hbm, gy_hbm,
           y_ref, xc_out, gc_out, h_out, da_out, db_out, p_out,
           x_v, gy_v, wg, wu, wd, xc, gc,
           pa, pb, pg, ra, rb, rg, sd, h, da, db,
           yp, s1, r1, s2, r2, sc, rc, yk, dxp,
           w_sem, o_sem, xs, xrs, gs, grs, es, ers, ys, yrs):
    rows, d_full = x_v.shape
    tok, d_half = xc.shape
    half = tok // 2
    nf = wg.shape[1] // FC
    nd = d_half // DC
    t = lax.axis_index("tp")
    c = lax.axis_index("dp")
    ty, tx = t // 2, t % 2
    tx_n = ty * 2 + 1 - tx
    ty_n = (1 - ty) * 2 + tx
    t_d = 3 - t
    t1 = (1 - c) * tx_n + c * ty_n
    t2 = (1 - c) * ty_n + c * tx_n
    order = ((t_d, c), (t_d, 1 - c), (tx_n, c), (tx_n, 1 - c), (ty_n, c), (ty_n, 1 - c), (t, 1 - c))

    def rows_of(q, chip):
        return pl.ds(pl.multiple_of((q * 4 + chip) * rows, rows), rows)

    def cols_of(q):
        return pl.ds(pl.multiple_of(q * d_half, d_half), d_half)

    cx = pltpu.make_async_copy(x_hbm, x_v, w_sem.at[0])
    cg = pltpu.make_async_copy(gy_hbm, gy_v, w_sem.at[1])
    cw = [pltpu.make_async_copy(a, b, w_sem.at[2 + i])
          for i, (a, b) in enumerate(((wg_hbm, wg), (wu_hbm, wu), (wd_hbm, wd)))]
    cx.start()
    cg.start()

    barrier = pltpu.get_barrier_semaphore()
    for chip, q in order:
        pl.semaphore_signal(barrier, inc=1, device_id={"tp": chip, "dp": q}, device_id_type=MESH)
    pl.semaphore_wait(barrier, 7)

    def remote(src, dst, ssem, rsem, chip, q):
        cp = pltpu.make_async_remote_copy(src_ref=src, dst_ref=dst, send_sem=ssem, recv_sem=rsem,
                                          device_id={"tp": chip, "dp": q}, device_id_type=MESH)
        cp.start()
        return cp

    def swap(src, dst, i):
        return remote(src, dst, es.at[i], ers.at[i], t, 1 - c)

    def spread(own, cols, ssem, rsem):
        return [remote(own.at[:, cols_of(q)], cols.at[rows_of(c, t), :], ssem.at[k], rsem.at[k], chip, q)
                for k, (chip, q) in enumerate(order)]

    cx.wait()
    sx = spread(x_v, xc, xs, xrs)
    for w in cw:
        w.start()
    xc[rows_of(c, t), :] = x_v[:, cols_of(c)]
    cg.wait()
    for cp in sx:
        cp.wait_send()
    sg = spread(gy_v, gc, gs, grs)
    gc[rows_of(c, t), :] = gy_v[:, cols_of(c)]

    mine = pl.multiple_of(c * half, half)
    theirs = pl.ds(pl.multiple_of((1 - c) * half, half), half)
    cw[0].wait()
    cw[1].wait()
    for cp in sx:
        cp.wait_recv()
    out_x = pltpu.make_async_copy(xc, xc_out, o_sem.at[0])
    out_x.start()
    cps = {}
    for j in range(nf):
        f = slice(j * FC, (j + 1) * FC)
        pa[j] = jnp.dot(xc[...], wg[:, f], preferred_element_type=F32)
        cps["a", j] = swap(pa.at[j, theirs, :], ra.at[j], 6 * j)
        pb[j] = jnp.dot(xc[...], wu[:, f], preferred_element_type=F32)
        cps["b", j] = swap(pb.at[j, theirs, :], rb.at[j], 6 * j + 1)

    def blocks():
        for i in range(0, half, RB):
            yield pl.ds(pl.multiple_of(mine + i, RB), RB), slice(i, i + RB)

    for j in range(nf):
        f = slice(j * FC, (j + 1) * FC)
        cps["a", j].wait_recv()
        cps["b", j].wait_recv()
        for r, i in blocks():
            a = pa[j, r, :] + ra[j, i, :]
            b = pb[j, r, :] + rb[j, i, :]
            s = jax.nn.sigmoid(a)
            u = a * s
            h[r, f] = (u * b).astype(BF16)
            sd[j, i, :] = s * (1.0 + a * (1.0 - s))
            ra[j, i, :] = u
            rb[j, i, :] = b
        own = h.at[pl.ds(mine, half), f]
        cps["h", j] = swap(own, own, 6 * j + 3)
    for j in range(nf):
        cps["h", j].wait_recv()

    def y_part(n):
        o = slice(n * DC, (n + 1) * DC)
        yp[:, o] = jnp.dot(h[...], wd[:, o], preferred_element_type=F32)
        for q in range(2):
            for e, chip in enumerate((t1, t_d)):
                s1[n, (q * 2 + e) * rows:(q * 2 + e + 1) * rows, :] = yp[rows_of(q, chip), o]
        cps["1", n] = remote(s1.at[n], r1.at[n], ys.at[4 * n], yrs.at[4 * n], t1, c)

    def y_step(n):
        o = slice(n * DC, (n + 1) * DC)
        cps["1", n].wait_recv()

        def got(q, e):
            return r1[n, pl.ds(pl.multiple_of((q * 2 + e) * rows, rows), rows), :]

        s2[n, 0] = yp[rows_of(c, t2), o] + got(c, 1)
        s2[n, 1] = yp[rows_of(1 - c, t2), o] + got(1 - c, 1)
        cps["2", n] = remote(s2.at[n, 0], r2.at[n, 0], ys.at[4 * n + 1], yrs.at[4 * n + 1], t2, c)
        cps["3", n] = remote(s2.at[n, 1], r2.at[n, 1], ys.at[4 * n + 2], yrs.at[4 * n + 2], t2, 1 - c)
        sc[n] = yp[rows_of(1 - c, t), o] + got(1 - c, 0)
        cps["4", n] = remote(sc.at[n], rc.at[n], ys.at[4 * n + 3], yrs.at[4 * n + 3], t, 1 - c)
        yk[n] = yp[rows_of(c, t), o] + got(c, 0)

    def y_done(n):
        for k in "234":
            cps[k, n].wait_recv()
        for q, tot in ((c, yk[n] + r2[n, 0]), (1 - c, rc[n] + r2[n, 1])):
            cols = pl.ds(pl.multiple_of(q * d_half + n * DC, DC), DC)
            y_ref[:, cols] = (x_v[:, cols].astype(F32) + tot).astype(BF16)

    def g_part(j):
        pg[j] = lax.dot_general(gc[...], wd[j * FC:(j + 1) * FC, :], NT, preferred_element_type=F32)
        cps["g", j] = swap(pg.at[j, theirs, :], rg.at[j], 6 * j + 2)

    def grad(j):
        f = slice(j * FC, (j + 1) * FC)
        cps["g", j].wait_recv()
        for r, i in blocks():
            g = pg[j, r, :] + rg[j, i, :]
            da[r, f] = (g * rb[j, i, :] * sd[j, i, :]).astype(BF16)
            db[r, f] = (g * ra[j, i, :]).astype(BF16)
        own = da.at[pl.ds(mine, half), f]
        cps["da", j] = swap(own, own, 6 * j + 4)
        own = db.at[pl.ds(mine, half), f]
        cps["db", j] = swap(own, own, 6 * j + 5)

    def dx_part(j):
        f = slice(j * FC, (j + 1) * FC)
        cps["da", j].wait_recv()
        cps["db", j].wait_recv()
        for n in range(nd):
            o = slice(n * DC, (n + 1) * DC)
            part = (lax.dot_general(da[:, f], wg[o, f], NT, preferred_element_type=F32)
                    + lax.dot_general(db[:, f], wu[o, f], NT, preferred_element_type=F32))
            dxp[:, o] = part if j == 0 else dxp[:, o] + part

    cw[2].wait()
    y_part(0)
    y_part(1)
    for cp in sg:
        cp.wait_recv()
    g_part(0)
    g_part(1)
    g_part(2)
    grad(0)
    g_part(3)
    grad(1)
    y_part(2)
    y_step(0)
    grad(2)
    dx_part(0)
    grad(3)
    dx_part(1)
    y_step(1)
    dx_part(2)
    y_step(2)
    dx_part(3)

    for i in range(8):
        r = ((i % 2) * 4 + i // 2) * rows
        p_out[i] = dxp[r:r + rows, :]
    for q in range(2):
        p_out[t * 2 + q] += gc[rows_of(q, t), :].astype(F32)
    gc_out[...] = gc[...]
    h_out[...] = h[...]
    da_out[...] = da[...]
    db_out[...] = db[...]
    for n in range(nd):
        y_done(n)

    for cp in sg:
        cp.wait_send()
    for cp in cps.values():
        cp.wait_send()
    out_x.wait()


def _finish(y_in, p, y_ref, dx_ref):
    d_half = p.shape[2]
    y_ref[...] = y_in[...]
    for q in range(2):
        dx_ref[:, q * d_half:(q + 1) * d_half] = (p[q] + p[q + 2] + p[q + 4] + p[q + 6]).astype(BF16)


def _grads(h, da, db, xc_hbm, gc, dwd_hbm, dwg_hbm, dwu_hbm, buf_d, buf_g, xc, sem_d, sem_g, sem_x):
    ff = h.shape[1]
    d_half = xc.shape[1]
    nb_d, tr_d = buf_d.shape[:2]
    nb_g, tr_g = buf_g.shape[:2]
    cx = pltpu.make_async_copy(xc_hbm, xc, sem_x)
    cx.start()

    def run(lhs, rhs, out, buf, sem, n, tr, nb, start, prev_out):
        def step(i, carry):
            slot = lax.rem(i + start, nb)
            r = pl.multiple_of(i * tr, tr)

            def drain():
                pltpu.make_async_copy(buf.at[slot], prev_out.at[pl.ds(0, tr), :], sem.at[slot]).wait()

            if start >= nb:
                drain()
            else:
                pl.when(i + start >= nb)(drain)
            buf[slot] = lax.dot_general(lhs[:, pl.ds(r, tr)], rhs[...], TN, preferred_element_type=F32)
            pltpu.make_async_copy(buf.at[slot], out.at[pl.ds(r, tr), :], sem.at[slot]).start()
            return carry

        lax.fori_loop(0, n, step, 0)

    n_d = ff // tr_d
    n_g = d_half // tr_g
    run(h, gc, dwd_hbm, buf_d, sem_d, n_d, tr_d, nb_d, 0, dwd_hbm)
    cx.wait()
    run(xc, da, dwg_hbm, buf_g, sem_g, n_g, tr_g, nb_g, 0, dwg_hbm)
    run(xc, db, dwu_hbm, buf_g, sem_g, n_g, tr_g, nb_g, n_g, dwu_hbm)
    for s in range(nb_d):
        pltpu.make_async_copy(buf_d.at[s], dwd_hbm.at[pl.ds(0, tr_d), :], sem_d.at[s]).wait()
    for s in range(nb_g):
        pltpu.make_async_copy(buf_g.at[s], dwu_hbm.at[pl.ds(0, tr_g), :], sem_g.at[s]).wait()


def solution(mesh):
    def local_step(x, wg, wu, wd, gy):
        rows, d_full = x.shape
        d_half, ff = wg.shape
        tok = rows * 8
        nf = ff // FC
        nd = d_half // DC
        any_ = pl.BlockSpec(memory_space=pl.ANY)
        hbm = pl.BlockSpec(memory_space=pltpu.HBM)
        vm = pl.BlockSpec(memory_space=pltpu.VMEM)
        S = jax.ShapeDtypeStruct
        dma = pltpu.SemaphoreType.DMA
        full = pltpu.VMEM((nf, tok, FC), F32)
        part = pltpu.VMEM((nf, tok // 2, FC), F32)
        block = pltpu.VMEM((nd, rows, DC), F32)
        y, xc, gc, h, da, db, parts = pl.pallas_call(
            _front,
            name="front",
            out_shape=(S((rows, d_full), BF16),
                       pltpu.HBM((tok, d_half), BF16), S((tok, d_half), BF16),
                       S((tok, ff), BF16), S((tok, ff), BF16), S((tok, ff), BF16))
            + (S((8, rows, d_half), F32),),
            in_specs=[hbm] * 5,
            out_specs=(vm, hbm, vm, vm, vm, vm, vm),
            scratch_shapes=[
                pltpu.VMEM((rows, d_full), BF16), pltpu.VMEM((rows, d_full), BF16),
                pltpu.VMEM((d_half, ff), BF16), pltpu.VMEM((d_half, ff), BF16), pltpu.VMEM((ff, d_half), BF16),
                pltpu.VMEM((tok, d_half), BF16), pltpu.VMEM((tok, d_half), BF16),
                full, full, full, part, part, part, part,
                pltpu.VMEM((tok, ff), BF16), pltpu.VMEM((tok, ff), BF16), pltpu.VMEM((tok, ff), BF16),
                pltpu.VMEM((tok, d_half), F32),
                pltpu.VMEM((nd, 4 * rows, DC), F32), pltpu.VMEM((nd, 4 * rows, DC), F32),
                pltpu.VMEM((nd, 2, rows, DC), F32), pltpu.VMEM((nd, 2, rows, DC), F32),
                block, block, block,
                pltpu.VMEM((tok, d_half), F32),
                dma((5,)), dma((1,)), dma((7,)), dma((7,)), dma((7,)), dma((7,)),
                dma((6 * nf,)), dma((6 * nf,)), dma((4 * nd,)), dma((4 * nd,)),
            ],
            compiler_params=pltpu.CompilerParams(collective_id=0, has_side_effects=True,
                                                 vmem_limit_bytes=50 * 1024 * 1024),
        )(*(pltpu.with_memory_space_constraint(v, pltpu.HBM) for v in (x, wg, wu, wd, gy)))
        parts = lax.all_to_all(parts, ("tp", "dp"), 0, 0, tiled=True)

        tr = 256
        dwd, dwg, dwu = pl.pallas_call(
            _grads,
            name="grads",
            out_shape=(S((ff, d_half), F32), S((d_half, ff), F32), S((d_half, ff), F32)),
            in_specs=[vm, vm, vm, hbm, vm],
            out_specs=(any_, any_, any_),
            scratch_shapes=[pltpu.VMEM((8, tr, d_half), F32), pltpu.VMEM((6, tr, ff), F32),
                            pltpu.VMEM((tok, d_half), BF16), dma((8,)), dma((6,)), dma(())],
            cost_estimate=pl.CostEstimate(flops=6 * tok * d_half * ff, bytes_accessed=12 * d_half * ff,
                                          transcendentals=0),
            compiler_params=pltpu.CompilerParams(vmem_limit_bytes=34 * 1024 * 1024),
        )(h, da, db, pltpu.with_memory_space_constraint(xc, pltpu.HBM), gc)
        y, dx = pl.pallas_call(
            _finish,
            name="finish",
            out_shape=(S((rows, d_full), BF16), S((rows, d_full), BF16)),
            in_specs=[vm] * 2,
            out_specs=(vm, vm),
            compiler_params=pltpu.CompilerParams(vmem_limit_bytes=6 * 1024 * 1024),
        )(y, parts)
        return y, dx, dwg, dwu, dwd

    row_spec = P(("dp", "tp"), None)
    up_spec = P("dp", "tp")
    down_spec = P("tp", "dp")
    return jax.shard_map(local_step, mesh=mesh,
                         in_specs=(row_spec, up_spec, up_spec, down_spec, row_spec),
                         out_specs=(row_spec, row_spec, up_spec, up_spec, down_spec),
                         check_vma=False)
```

time: 45.8 us -> 45 us (0.983)
  waiting for transfers between devices: 2.58 us -> 0.01 us
  Pallas kernels: 40.1 us -> 41.7 us
    all_to_all x1, waiting for transfers between devices: 2.58 us -> 0.01 us  [local_step(): parts = lax.all_to_all(parts, ('tp', 'dp'), 0, 0, tiled=True)]
    pallas_call x1, Pallas kernels: 26.7 us -> 28.3 us  [local_step(): pl.pallas_call(_front, name='front', out_shape=(S((rows, d_full), BF16),...]
  transfers between devices with their start and end apart: 1 -> 1, of which waited for: 1 -> 0; matrix products, arithmetic and copies ran while one was open for 0% -> 0% of each run, Pallas kernels for 28% -> 28%
where the time goes in v5:
time: 45 us; the launch traced here: 44.8 us
  Pallas kernels  41.7 us (93%)
  starting transfers between devices  2.5 us (6%)
  between operations  0.66 us (1%)
    pallas_call x1, Pallas kernels, local_step(): pl.pallas_call(_front, name='front', out_shape=(S((rows, d_full), BF16),...  28.3 us
    pallas_call x1, Pallas kernels, local_step(): pl.pallas_call(_grads, name='grads', out_shape=(S((ff, d_half), F32), S((...  12.7 us
    all_to_all x1, starting transfers between devices, local_step(): parts = lax.all_to_all(parts, ('tp', 'dp'), 0, 0, tiled=True)  2.5 us
  transfers between devices with their start and end apart: 1, of which 0 were waited for; matrix products, arithmetic and copies ran while one was open for 0% of the time, Pallas kernels for 28%

profile of v5, /device:TPU:0, one launch (start us, length us, event | category | flops | bytes accessed | tf_op | source)
XLA Modules:
  0.0 44.8 jit_solution(8353755306408470)
XLA Ops:
  0.6 28.3 %front.1 = (bf16[16,3072]{1,0:T(8,128)(2,1)S(1)}, bf16[128,1536]{1,0:T(8,128)(2,1)}, bf16[128,1536]{1,0:T(8,128)(2,1)S(1)}, bf16[128,2048]{1,0:T(8,128)(2,1)S(1)...) custom-call(bf16[16,3072]{1,0:T(8,128)(2,1)} %x_hbm.1, ...), custom_call_target="tpu_custom_call" | custom-call | tf_op jit(solution)/shard_map/front/pallas_call | solution.py:280
  28.9 2.5 %all-to-all-start = ((f32[8,16,1536]{2,1,0:T(8,128)}), f32[8,16,1536]{2,1,0:T(8,128)S(1)}, u32[]{:S(2)}, u32[]{:S(2)}) async-start(f32[8,16,1536]{2,1,0:T(8,128)} %get-tuple-element.18), calls=%async_computation | async-start | bytes 1572864 | tf_op jit(solution)/shard_map/all_to_all | solution.py:306
  31.4 12.7 %grads.1 = (f32[2048,1536]{1,0:T(8,128)}, f32[1536,2048]{1,0:T(8,128)}, f32[1536,2048]{1,0:T(8,128)}) custom-call(bf16[128,2048]{1,0:T(8,128)(2,1)S(1)} %get-tuple-element.21.h, bf16[128,2048]{1,0:T(8,128)(2,1)S(1)} %get-tuple-element.22.da, bf16[128,2048]{1,0:T(8,128)(2,1)S(1)} %get-tuple-element.23.db, bf16[128,1536]{1,0:T(8,128)(2,1)} %get-tuple-element.24.xc_hbm, ...), custom_call_target="tpu_custom_call" | custom-call | flops 2415919104 | bytes 37748736 | tf_op jit(solution)/shard_map/grads/pallas_call | solution.py:309
  44.1 0.0 all-to-all-done.p
  44.1 0.7 %finish.1 = (bf16[16,3072]{1,0:T(8,128)(2,1)}, bf16[16,3072]{1,0:T(8,128)(2,1)}) custom-call(bf16[16,3072]{1,0:T(8,128)(2,1)S(1)} %get-tuple-element.17.y_in, f32[8,16,1536]{2,1,0:T(8,128)S(1)} %all-to-all-done.p), custom_call_target="tpu_custom_call" | custom-call | tf_op jit(solution)/shard_map/finish/pallas_call | solution.py:321
Async XLA Ops:
  28.9 15.2 %all-to-all-start = ((f32[8,16,1536]{2,1,0:T(8,128)}), f32[8,16,1536]{2,1,0:T(8,128)S(1)}, u32[]{:S(2)}, u32[]{:S(2)}) async-start(f32[8,16,1536]{2,1,0:T(8,128)} %get-tuple-element.18), calls=%async_computation | async-start | bytes 1572864 | tf_op jit(solution)/shard_map/all_to_all | solution.py:306

commit v6 on v5

--- a/solution.py
+++ b/solution.py
@@ -52,6 +52,8 @@
           for i, (a, b) in enumerate(((wg_hbm, wg), (wu_hbm, wu), (wd_hbm, wd)))]
     cx.start()
     cg.start()
+    for w in cw:
+        w.start()
 
     barrier = pltpu.get_barrier_semaphore()
     for chip, q in order:
@@ -73,8 +75,6 @@
 
     cx.wait()
     sx = spread(x_v, xc, xs, xrs)
-    for w in cw:
-        w.start()
     xc[rows_of(c, t), :] = x_v[:, cols_of(c)]
     cg.wait()
     for cp in sx:
@@ -117,9 +117,6 @@
             rb[j, i, :] = b
         own = h.at[pl.ds(mine, half), f]
         cps["h", j] = swap(own, own, 6 * j + 3)
-    for j in range(nf):
-        cps["h", j].wait_recv()
-
     def y_part(n):
         o = slice(n * DC, (n + 1) * DC)
         yp[:, o] = jnp.dot(h[...], wd[:, o], preferred_element_type=F32)
@@ -177,21 +174,23 @@
             dxp[:, o] = part if j == 0 else dxp[:, o] + part
 
     cw[2].wait()
-    y_part(0)
-    y_part(1)
     for cp in sg:
         cp.wait_recv()
     g_part(0)
     g_part(1)
+    for j in range(nf):
+        cps["h", j].wait_recv()
+    y_part(0)
+    y_part(1)
+    y_part(2)
     g_part(2)
     grad(0)
     g_part(3)
     grad(1)
-    y_part(2)
-    y_step(0)
     grad(2)
     dx_part(0)
     grad(3)
+    y_step(0)
     dx_part(1)
     y_step(1)
     dx_part(2)

time: 45 us -> 45 us (level)
  no operation moved by 1% of the time
where the time goes in v6:
time: 45 us; the launch traced here: 44.8 us
  Pallas kernels  41.8 us (93%)
  starting transfers between devices  2.34 us (5%)
  between operations  0.66 us (1%)
    pallas_call x1, Pallas kernels, local_step(): pl.pallas_call(_front, name='front', out_shape=(S((rows, d_full), BF16),...  28.4 us
    pallas_call x1, Pallas kernels, local_step(): pl.pallas_call(_grads, name='grads', out_shape=(S((ff, d_half), F32), S((...  12.7 us
    all_to_all x1, starting transfers between devices, local_step(): parts = lax.all_to_all(parts, ('tp', 'dp'), 0, 0, tiled=True)  2.34 us
  transfers between devices with their start and end apart: 1, of which 0 were waited for; matrix products, arithmetic and copies ran while one was open for 0% of the time, Pallas kernels for 28%

profile of v6, /device:TPU:0, one launch (start us, length us, event | category | flops | bytes accessed | tf_op | source)
XLA Modules:
  0.0 44.8 jit_solution(9555365296576042387)
XLA Ops:
  0.6 28.4 %front.1 = (bf16[16,3072]{1,0:T(8,128)(2,1)S(1)}, bf16[128,1536]{1,0:T(8,128)(2,1)}, bf16[128,1536]{1,0:T(8,128)(2,1)S(1)}, bf16[128,2048]{1,0:T(8,128)(2,1)S(1)...) custom-call(bf16[16,3072]{1,0:T(8,128)(2,1)} %x_hbm.1, ...), custom_call_target="tpu_custom_call" | custom-call | tf_op jit(solution)/shard_map/front/pallas_call | solution.py:279
  29.0 2.3 %all-to-all-start = ((f32[8,16,1536]{2,1,0:T(8,128)}), f32[8,16,1536]{2,1,0:T(8,128)S(1)}, u32[]{:S(2)}, u32[]{:S(2)}) async-start(f32[8,16,1536]{2,1,0:T(8,128)} %get-tuple-element.18), calls=%async_computation | async-start | bytes 1572864 | tf_op jit(solution)/shard_map/all_to_all | solution.py:305
  31.4 12.7 %grads.1 = (f32[2048,1536]{1,0:T(8,128)}, f32[1536,2048]{1,0:T(8,128)}, f32[1536,2048]{1,0:T(8,128)}) custom-call(bf16[128,2048]{1,0:T(8,128)(2,1)S(1)} %get-tuple-element.21.h, bf16[128,2048]{1,0:T(8,128)(2,1)S(1)} %get-tuple-element.22.da, bf16[128,2048]{1,0:T(8,128)(2,1)S(1)} %get-tuple-element.23.db, bf16[128,1536]{1,0:T(8,128)(2,1)} %get-tuple-element.24.xc_hbm, ...), custom_call_target="tpu_custom_call" | custom-call | flops 2415919104 | bytes 37748736 | tf_op jit(solution)/shard_map/grads/pallas_call | solution.py:308
  44.1 0.0 all-to-all-done.p
  44.1 0.7 %finish.1 = (bf16[16,3072]{1,0:T(8,128)(2,1)}, bf16[16,3072]{1,0:T(8,128)(2,1)}) custom-call(bf16[16,3072]{1,0:T(8,128)(2,1)S(1)} %get-tuple-element.17.y_in, f32[8,16,1536]{2,1,0:T(8,128)S(1)} %all-to-all-done.p), custom_call_target="tpu_custom_call" | custom-call | tf_op jit(solution)/shard_map/finish/pallas_call | solution.py:320
Async XLA Ops:
  29.0 15.0 %all-to-all-start = ((f32[8,16,1536]{2,1,0:T(8,128)}), f32[8,16,1536]{2,1,0:T(8,128)S(1)}, u32[]{:S(2)}, u32[]{:S(2)}) async-start(f32[8,16,1536]{2,1,0:T(8,128)} %get-tuple-element.18), calls=%async_computation | async-start | bytes 1572864 | tf_op jit(solution)/shard_map/all_to_all | solution.py:305

commit v7 on v5

--- a/solution.py
+++ b/solution.py
@@ -16,6 +16,7 @@
 
 FC = 512
 DC = 512
+SPLIT = 2
 RB = 32
 
 
@@ -52,6 +53,8 @@
           for i, (a, b) in enumerate(((wg_hbm, wg), (wu_hbm, wu), (wd_hbm, wd)))]
     cx.start()
     cg.start()
+    for w in cw:
+        w.start()
 
     barrier = pltpu.get_barrier_semaphore()
     for chip, q in order:
@@ -73,8 +76,6 @@
 
     cx.wait()
     sx = spread(x_v, xc, xs, xrs)
-    for w in cw:
-        w.start()
     xc[rows_of(c, t), :] = x_v[:, cols_of(c)]
     cg.wait()
     for cp in sx:
@@ -91,22 +92,28 @@
     out_x = pltpu.make_async_copy(xc, xc_out, o_sem.at[0])
     out_x.start()
     cps = {}
+
+    def swap_part(part, got, j, i):
+        if j < SPLIT:
+            return swap(part.at[j, theirs, :], got.at[j, pl.ds(0, half), :], i)
+        return swap(part.at[j], got.at[j], i)
+
     for j in range(nf):
         f = slice(j * FC, (j + 1) * FC)
         pa[j] = jnp.dot(xc[...], wg[:, f], preferred_element_type=F32)
-        cps["a", j] = swap(pa.at[j, theirs, :], ra.at[j], 6 * j)
+        cps["a", j] = swap_part(pa, ra, j, 6 * j)
         pb[j] = jnp.dot(xc[...], wu[:, f], preferred_element_type=F32)
-        cps["b", j] = swap(pb.at[j, theirs, :], rb.at[j], 6 * j + 1)
-
-    def blocks():
-        for i in range(0, half, RB):
-            yield pl.ds(pl.multiple_of(mine + i, RB), RB), slice(i, i + RB)
+        cps["b", j] = swap_part(pb, rb, j, 6 * j + 1)
+
+    def blocks(j):
+        for i in range(0, half if j < SPLIT else tok, RB):
+            yield pl.ds(pl.multiple_of(mine + i, RB), RB) if j < SPLIT else slice(i, i + RB), slice(i, i + RB)
 
     for j in range(nf):
         f = slice(j * FC, (j + 1) * FC)
         cps["a", j].wait_recv()
         cps["b", j].wait_recv()
-        for r, i in blocks():
+        for r, i in blocks(j):
             a = pa[j, r, :] + ra[j, i, :]
             b = pb[j, r, :] + rb[j, i, :]
             s = jax.nn.sigmoid(a)
@@ -115,11 +122,9 @@
             sd[j, i, :] = s * (1.0 + a * (1.0 - s))
             ra[j, i, :] = u
             rb[j, i, :] = b
-        own = h.at[pl.ds(mine, half), f]
-        cps["h", j] = swap(own, own, 6 * j + 3)
-    for j in range(nf):
-        cps["h", j].wait_recv()
-
+        if j < SPLIT:
+            own = h.at[pl.ds(mine, half), f]
+            cps["h", j] = swap(own, own, 6 * j + 3)
     def y_part(n):
         o = slice(n * DC, (n + 1) * DC)
         yp[:, o] = jnp.dot(h[...], wd[:, o], preferred_element_type=F32)
@@ -152,24 +157,26 @@
 
     def g_part(j):
         pg[j] = lax.dot_general(gc[...], wd[j * FC:(j + 1) * FC, :], NT, preferred_element_type=F32)
-        cps["g", j] = swap(pg.at[j, theirs, :], rg.at[j], 6 * j + 2)
+        cps["g", j] = swap_part(pg, rg, j, 6 * j + 2)
 
     def grad(j):
         f = slice(j * FC, (j + 1) * FC)
         cps["g", j].wait_recv()
-        for r, i in blocks():
+        for r, i in blocks(j):
             g = pg[j, r, :] + rg[j, i, :]
             da[r, f] = (g * rb[j, i, :] * sd[j, i, :]).astype(BF16)
             db[r, f] = (g * ra[j, i, :]).astype(BF16)
-        own = da.at[pl.ds(mine, half), f]
-        cps["da", j] = swap(own, own, 6 * j + 4)
-        own = db.at[pl.ds(mine, half), f]
-        cps["db", j] = swap(own, own, 6 * j + 5)
+        if j < SPLIT:
+            own = da.at[pl.ds(mine, half), f]
+            cps["da", j] = swap(own, own, 6 * j + 4)
+            own = db.at[pl.ds(mine, half), f]
+            cps["db", j] = swap(own, own, 6 * j + 5)
 
     def dx_part(j):
         f = slice(j * FC, (j + 1) * FC)
-        cps["da", j].wait_recv()
-        cps["db", j].wait_recv()
+        if j < SPLIT:
+            cps["da", j].wait_recv()
+            cps["db", j].wait_recv()
         for n in range(nd):
             o = slice(n * DC, (n + 1) * DC)
             part = (lax.dot_general(da[:, f], wg[o, f], NT, preferred_element_type=F32)
@@ -177,8 +184,11 @@
             dxp[:, o] = part if j == 0 else dxp[:, o] + part
 
     cw[2].wait()
+    for j in range(SPLIT):
+        cps["h", j].wait_recv()
     y_part(0)
     y_part(1)
+    y_part(2)
     for cp in sg:
         cp.wait_recv()
     g_part(0)
@@ -187,12 +197,11 @@
     grad(0)
     g_part(3)
     grad(1)
-    y_part(2)
+    dx_part(0)
     y_step(0)
     grad(2)
-    dx_part(0)
+    dx_part(1)
     grad(3)
-    dx_part(1)
     y_step(1)
     dx_part(2)
     y_step(2)
@@ -275,7 +284,6 @@
         S = jax.ShapeDtypeStruct
         dma = pltpu.SemaphoreType.DMA
         full = pltpu.VMEM((nf, tok, FC), F32)
-        part = pltpu.VMEM((nf, tok // 2, FC), F32)
         block = pltpu.VMEM((nd, rows, DC), F32)
         y, xc, gc, h, da, db, parts = pl.pallas_call(
             _front,
@@ -290,7 +298,7 @@
                 pltpu.VMEM((rows, d_full), BF16), pltpu.VMEM((rows, d_full), BF16),
                 pltpu.VMEM((d_half, ff), BF16), pltpu.VMEM((d_half, ff), BF16), pltpu.VMEM((ff, d_half), BF16),
                 pltpu.VMEM((tok, d_half), BF16), pltpu.VMEM((tok, d_half), BF16),
-                full, full, full, part, part, part, part,
+                full, full, full, full, full, full, full,
                 pltpu.VMEM((tok, ff), BF16), pltpu.VMEM((tok, ff), BF16), pltpu.VMEM((tok, ff), BF16),
                 pltpu.VMEM((tok, d_half), F32),
                 pltpu.VMEM((nd, 4 * rows, DC), F32), pltpu.VMEM((nd, 4 * rows, DC), F32),

time: 45 us -> 44.2 us (0.982)
  Pallas kernels: 41.7 us -> 41.1 us
    pallas_call x1, Pallas kernels: 28.3 us -> 27.7 us  [local_step(): pl.pallas_call(_front, name='front', out_shape=(S((rows, d_full), BF16),...]
  transfers between devices with their start and end apart: 1 -> 1, of which waited for: 0 -> 0; matrix products, arithmetic and copies ran while one was open for 0% -> 0% of each run, Pallas kernels for 28% -> 29%
where the time goes in v7:
time: 44.2 us; the launch traced here: 44.1 us
  Pallas kernels  41.1 us (93%)
  starting transfers between devices  2.3 us (5%)
  between operations  0.66 us (1%)
    pallas_call x1, Pallas kernels, local_step(): pl.pallas_call(_front, name='front', out_shape=(S((rows, d_full), BF16),...  27.7 us
    pallas_call x1, Pallas kernels, local_step(): pl.pallas_call(_grads, name='grads', out_shape=(S((ff, d_half), F32), S((...  12.7 us
    all_to_all x1, starting transfers between devices, local_step(): parts = lax.all_to_all(parts, ('tp', 'dp'), 0, 0, tiled=True)  2.3 us
  transfers between devices with their start and end apart: 1, of which 0 were waited for; matrix products, arithmetic and copies ran while one was open for 0% of the time, Pallas kernels for 29%

profile of v7, /device:TPU:0, one launch (start us, length us, event | category | flops | bytes accessed | tf_op | source)
XLA Modules:
  0.0 44.1 jit_solution(1912316448107583648)
XLA Ops:
  0.6 27.7 %front.1 = (bf16[16,3072]{1,0:T(8,128)(2,1)S(1)}, bf16[128,1536]{1,0:T(8,128)(2,1)}, bf16[128,1536]{1,0:T(8,128)(2,1)S(1)}, bf16[128,2048]{1,0:T(8,128)(2,1)S(1)...) custom-call(bf16[16,3072]{1,0:T(8,128)(2,1)} %x_hbm.1, ...), custom_call_target="tpu_custom_call" | custom-call | tf_op jit(solution)/shard_map/front/pallas_call | solution.py:288
  28.3 2.3 %all-to-all-start = ((f32[8,16,1536]{2,1,0:T(8,128)}), f32[8,16,1536]{2,1,0:T(8,128)S(1)}, u32[]{:S(2)}, u32[]{:S(2)}) async-start(f32[8,16,1536]{2,1,0:T(8,128)} %get-tuple-element.18), calls=%async_computation | async-start | bytes 1572864 | tf_op jit(solution)/shard_map/all_to_all | solution.py:314
  30.6 12.7 %grads.1 = (f32[2048,1536]{1,0:T(8,128)}, f32[1536,2048]{1,0:T(8,128)}, f32[1536,2048]{1,0:T(8,128)}) custom-call(bf16[128,2048]{1,0:T(8,128)(2,1)S(1)} %get-tuple-element.21.h, bf16[128,2048]{1,0:T(8,128)(2,1)S(1)} %get-tuple-element.22.da, bf16[128,2048]{1,0:T(8,128)(2,1)S(1)} %get-tuple-element.23.db, bf16[128,1536]{1,0:T(8,128)(2,1)} %get-tuple-element.24.xc_hbm, ...), custom_call_target="tpu_custom_call" | custom-call | flops 2415919104 | bytes 37748736 | tf_op jit(solution)/shard_map/grads/pallas_call | solution.py:317
  43.3 0.0 all-to-all-done.p
  43.3 0.7 %finish.1 = (bf16[16,3072]{1,0:T(8,128)(2,1)}, bf16[16,3072]{1,0:T(8,128)(2,1)}) custom-call(bf16[16,3072]{1,0:T(8,128)(2,1)S(1)} %get-tuple-element.17.y_in, f32[8,16,1536]{2,1,0:T(8,128)S(1)} %all-to-all-done.p), custom_call_target="tpu_custom_call" | custom-call | tf_op jit(solution)/shard_map/finish/pallas_call | solution.py:329
Async XLA Ops:
  28.3 15.0 %all-to-all-start = ((f32[8,16,1536]{2,1,0:T(8,128)}), f32[8,16,1536]{2,1,0:T(8,128)S(1)}, u32[]{:S(2)}, u32[]{:S(2)}) async-start(f32[8,16,1536]{2,1,0:T(8,128)} %get-tuple-element.18), calls=%async_computation | async-start | bytes 1572864 | tf_op jit(solution)/shard_map/all_to_all | solution.py:314

commit v8 on v7

--- a/solution.py
+++ b/solution.py
@@ -197,14 +197,14 @@
     grad(0)
     g_part(3)
     grad(1)
+    y_step(0)
     dx_part(0)
-    y_step(0)
     grad(2)
+    y_step(1)
     dx_part(1)
     grad(3)
-    y_step(1)
+    y_step(2)
     dx_part(2)
-    y_step(2)
     dx_part(3)
 
     for i in range(8):
@@ -313,15 +313,15 @@
         )(*(pltpu.with_memory_space_constraint(v, pltpu.HBM) for v in (x, wg, wu, wd, gy)))
         parts = lax.all_to_all(parts, ("tp", "dp"), 0, 0, tiled=True)
 
-        tr = 256
+        tr = 128
         dwd, dwg, dwu = pl.pallas_call(
             _grads,
             name="grads",
             out_shape=(S((ff, d_half), F32), S((d_half, ff), F32), S((d_half, ff), F32)),
             in_specs=[vm, vm, vm, hbm, vm],
             out_specs=(any_, any_, any_),
-            scratch_shapes=[pltpu.VMEM((8, tr, d_half), F32), pltpu.VMEM((6, tr, ff), F32),
-                            pltpu.VMEM((tok, d_half), BF16), dma((8,)), dma((6,)), dma(())],
+            scratch_shapes=[pltpu.VMEM((16, tr, d_half), F32), pltpu.VMEM((12, tr, ff), F32),
+                            pltpu.VMEM((tok, d_half), BF16), dma((16,)), dma((12,)), dma(())],
             cost_estimate=pl.CostEstimate(flops=6 * tok * d_half * ff, bytes_accessed=12 * d_half * ff,
                                           transcendentals=0),
             compiler_params=pltpu.CompilerParams(vmem_limit_bytes=34 * 1024 * 1024),

time: 44.2 us -> 44.9 us (1.016)
    pallas_call x1, Pallas kernels: 12.7 us -> 13.7 us  [local_step(): pl.pallas_call(_grads, name='grads', out_shape=(S((ff, d_half), F32), S((...]
    pallas_call x1, Pallas kernels: 27.7 us -> 27.1 us  [local_step(): pl.pallas_call(_front, name='front', out_shape=(S((rows, d_full), BF16),...]
  transfers between devices with their start and end apart: 1 -> 1, of which waited for: 0 -> 0; matrix products, arithmetic and copies ran while one was open for 0% -> 0% of each run, Pallas kernels for 29% -> 31%
where the time goes in v8:
time: 44.9 us; the launch traced here: 44.8 us
  Pallas kernels  41.4 us (92%)
  starting transfers between devices  2.7 us (6%)
  between operations  0.66 us (1%)
    pallas_call x1, Pallas kernels, local_step(): pl.pallas_call(_front, name='front', out_shape=(S((rows, d_full), BF16),...  27.1 us
    pallas_call x1, Pallas kernels, local_step(): pl.pallas_call(_grads, name='grads', out_shape=(S((ff, d_half), F32), S((...  13.7 us
    all_to_all x1, starting transfers between devices, local_step(): parts = lax.all_to_all(parts, ('tp', 'dp'), 0, 0, tiled=True)  2.7 us
  transfers between devices with their start and end apart: 1, of which 0 were waited for; matrix products, arithmetic and copies ran while one was open for 0% of the time, Pallas kernels for 31%

profile of v8, /device:TPU:0, one launch (start us, length us, event | category | flops | bytes accessed | tf_op | source)
XLA Modules:
  0.0 44.8 jit_solution(18324619459993988920)
XLA Ops:
  0.6 27.1 %front.1 = (bf16[16,3072]{1,0:T(8,128)(2,1)S(1)}, bf16[128,1536]{1,0:T(8,128)(2,1)}, bf16[128,1536]{1,0:T(8,128)(2,1)S(1)}, bf16[128,2048]{1,0:T(8,128)(2,1)S(1)...) custom-call(bf16[16,3072]{1,0:T(8,128)(2,1)} %x_hbm.1, ...), custom_call_target="tpu_custom_call" | custom-call | tf_op jit(solution)/shard_map/front/pallas_call | solution.py:288
  27.7 2.7 %all-to-all-start = ((f32[8,16,1536]{2,1,0:T(8,128)}), f32[8,16,1536]{2,1,0:T(8,128)S(1)}, u32[]{:S(2)}, u32[]{:S(2)}) async-start(f32[8,16,1536]{2,1,0:T(8,128)} %get-tuple-element.18), calls=%async_computation | async-start | bytes 1572864 | tf_op jit(solution)/shard_map/all_to_all | solution.py:314
  30.4 13.7 %grads.1 = (f32[2048,1536]{1,0:T(8,128)}, f32[1536,2048]{1,0:T(8,128)}, f32[1536,2048]{1,0:T(8,128)}) custom-call(bf16[128,2048]{1,0:T(8,128)(2,1)S(1)} %get-tuple-element.21.h, bf16[128,2048]{1,0:T(8,128)(2,1)S(1)} %get-tuple-element.22.da, bf16[128,2048]{1,0:T(8,128)(2,1)S(1)} %get-tuple-element.23.db, bf16[128,1536]{1,0:T(8,128)(2,1)} %get-tuple-element.24.xc_hbm, ...), custom_call_target="tpu_custom_call" | custom-call | flops 2415919104 | bytes 37748736 | tf_op jit(solution)/shard_map/grads/pallas_call | solution.py:317
  44.1 0.0 all-to-all-done.p
  44.1 0.7 %finish.1 = (bf16[16,3072]{1,0:T(8,128)(2,1)}, bf16[16,3072]{1,0:T(8,128)(2,1)}) custom-call(bf16[16,3072]{1,0:T(8,128)(2,1)S(1)} %get-tuple-element.17.y_in, f32[8,16,1536]{2,1,0:T(8,128)S(1)} %all-to-all-done.p), custom_call_target="tpu_custom_call" | custom-call | tf_op jit(solution)/shard_map/finish/pallas_call | solution.py:329
Async XLA Ops:
  27.7 16.4 %all-to-all-start = ((f32[8,16,1536]{2,1,0:T(8,128)}), f32[8,16,1536]{2,1,0:T(8,128)S(1)}, u32[]{:S(2)}, u32[]{:S(2)}) async-start(f32[8,16,1536]{2,1,0:T(8,128)} %get-tuple-element.18), calls=%async_computation | async-start | bytes 1572864 | tf_op jit(solution)/shard_map/all_to_all | solution.py:314

commit v9 on v8

--- a/solution.py
+++ b/solution.py
@@ -16,7 +16,7 @@
 
 FC = 512
 DC = 512
-SPLIT = 2
+SPLIT = 3
 RB = 32
 
 
@@ -313,18 +313,18 @@
         )(*(pltpu.with_memory_space_constraint(v, pltpu.HBM) for v in (x, wg, wu, wd, gy)))
         parts = lax.all_to_all(parts, ("tp", "dp"), 0, 0, tiled=True)
 
-        tr = 128
+        tr = 512
         dwd, dwg, dwu = pl.pallas_call(
             _grads,
             name="grads",
             out_shape=(S((ff, d_half), F32), S((d_half, ff), F32), S((d_half, ff), F32)),
             in_specs=[vm, vm, vm, hbm, vm],
             out_specs=(any_, any_, any_),
-            scratch_shapes=[pltpu.VMEM((16, tr, d_half), F32), pltpu.VMEM((12, tr, ff), F32),
-                            pltpu.VMEM((tok, d_half), BF16), dma((16,)), dma((12,)), dma(())],
+            scratch_shapes=[pltpu.VMEM((4, tr, d_half), F32), pltpu.VMEM((6, tr, ff), F32),
+                            pltpu.VMEM((tok, d_half), BF16), dma((4,)), dma((6,)), dma(())],
             cost_estimate=pl.CostEstimate(flops=6 * tok * d_half * ff, bytes_accessed=12 * d_half * ff,
                                           transcendentals=0),
-            compiler_params=pltpu.CompilerParams(vmem_limit_bytes=34 * 1024 * 1024),
+            compiler_params=pltpu.CompilerParams(vmem_limit_bytes=50 * 1024 * 1024),
         )(h, da, db, pltpu.with_memory_space_constraint(xc, pltpu.HBM), gc)
         y, dx = pl.pallas_call(
             _finish,

time: 44.9 us -> 44.5 us (level)
    pallas_call x1, Pallas kernels: 13.7 us -> 13 us  [local_step(): pl.pallas_call(_grads, name='grads', out_shape=(S((ff, d_half), F32), S((...]
  transfers between devices with their start and end apart: 1 -> 1, of which waited for: 0 -> 0; matrix products, arithmetic and copies ran while one was open for 0% -> 0% of each run, Pallas kernels for 31% -> 29%
where the time goes in v9:
time: 44.5 us; the launch traced here: 44.3 us
  Pallas kernels  41 us (92%)
  starting transfers between devices  2.69 us (6%)
  between operations  0.66 us (1%)
    pallas_call x1, Pallas kernels, local_step(): pl.pallas_call(_front, name='front', out_shape=(S((rows, d_full), BF16),...  27.3 us
    pallas_call x1, Pallas kernels, local_step(): pl.pallas_call(_grads, name='grads', out_shape=(S((ff, d_half), F32), S((...  13 us
    all_to_all x1, starting transfers between devices, local_step(): parts = lax.all_to_all(parts, ('tp', 'dp'), 0, 0, tiled=True)  2.69 us
  transfers between devices with their start and end apart: 1, of which 0 were waited for; matrix products, arithmetic and copies ran while one was open for 0% of the time, Pallas kernels for 29%

profile of v9, /device:TPU:0, one launch (start us, length us, event | category | flops | bytes accessed | tf_op | source)
XLA Modules:
  0.0 44.3 jit_solution(2074783102809955496)
XLA Ops:
  0.6 27.3 %front.1 = (bf16[16,3072]{1,0:T(8,128)(2,1)S(1)}, bf16[128,1536]{1,0:T(8,128)(2,1)}, bf16[128,1536]{1,0:T(8,128)(2,1)S(1)}, bf16[128,2048]{1,0:T(8,128)(2,1)S(1)...) custom-call(bf16[16,3072]{1,0:T(8,128)(2,1)} %x_hbm.1, ...), custom_call_target="tpu_custom_call" | custom-call | tf_op jit(solution)/shard_map/front/pallas_call | solution.py:288
  27.9 2.7 %all-to-all-start = ((f32[8,16,1536]{2,1,0:T(8,128)}), f32[8,16,1536]{2,1,0:T(8,128)S(1)}, u32[]{:S(2)}, u32[]{:S(2)}) async-start(f32[8,16,1536]{2,1,0:T(8,128)} %get-tuple-element.18), calls=%async_computation | async-start | bytes 1572864 | tf_op jit(solution)/shard_map/all_to_all | solution.py:314
  30.6 13.0 %grads.1 = (f32[2048,1536]{1,0:T(8,128)}, f32[1536,2048]{1,0:T(8,128)}, f32[1536,2048]{1,0:T(8,128)}) custom-call(bf16[128,2048]{1,0:T(8,128)(2,1)S(1)} %get-tuple-element.21.h, bf16[128,2048]{1,0:T(8,128)(2,1)S(1)} %get-tuple-element.22.da, bf16[128,2048]{1,0:T(8,128)(2,1)S(1)} %get-tuple-element.23.db, bf16[128,1536]{1,0:T(8,128)(2,1)} %get-tuple-element.24.xc_hbm, ...), custom_call_target="tpu_custom_call" | custom-call | flops 2415919104 | bytes 37748736 | tf_op jit(solution)/shard_map/grads/pallas_call | solution.py:317
  43.6 0.0 all-to-all-done.p
  43.6 0.7 %finish.1 = (bf16[16,3072]{1,0:T(8,128)(2,1)}, bf16[16,3072]{1,0:T(8,128)(2,1)}) custom-call(bf16[16,3072]{1,0:T(8,128)(2,1)S(1)} %get-tuple-element.17.y_in, f32[8,16,1536]{2,1,0:T(8,128)S(1)} %all-to-all-done.p), custom_call_target="tpu_custom_call" | custom-call | tf_op jit(solution)/shard_map/finish/pallas_call | solution.py:329
Async XLA Ops:
  27.9 15.7 %all-to-all-start = ((f32[8,16,1536]{2,1,0:T(8,128)}), f32[8,16,1536]{2,1,0:T(8,128)S(1)}, u32[]{:S(2)}, u32[]{:S(2)}) async-start(f32[8,16,1536]{2,1,0:T(8,128)} %get-tuple-element.18), calls=%async_computation | async-start | bytes 1572864 | tf_op jit(solution)/shard_map/all_to_all | solution.py:314

commit v10 on v8

--- a/solution.py
+++ b/solution.py
@@ -16,6 +16,8 @@
 
 FC = 512
 DC = 512
+PIECES = ((0, 512), (512, 512), (1024, 256), (1280, 128))
+FRONT = 1408
 SPLIT = 2
 RB = 32
 
@@ -125,34 +127,37 @@
         if j < SPLIT:
             own = h.at[pl.ds(mine, half), f]
             cps["h", j] = swap(own, own, 6 * j + 3)
-    def y_part(n):
+    def y_part(n, pieces):
         o = slice(n * DC, (n + 1) * DC)
         yp[:, o] = jnp.dot(h[...], wd[:, o], preferred_element_type=F32)
-        for q in range(2):
-            for e, chip in enumerate((t1, t_d)):
-                s1[n, (q * 2 + e) * rows:(q * 2 + e + 1) * rows, :] = yp[rows_of(q, chip), o]
-        cps["1", n] = remote(s1.at[n], r1.at[n], ys.at[4 * n], yrs.at[4 * n], t1, c)
-
-    def y_step(n):
-        o = slice(n * DC, (n + 1) * DC)
-        cps["1", n].wait_recv()
+        for p in pieces:
+            o = slice(PIECES[p][0], sum(PIECES[p]))
+            for q in range(2):
+                for e, chip in enumerate((t1, t_d)):
+                    s1[p][(q * 2 + e) * rows:(q * 2 + e + 1) * rows, :] = yp[rows_of(q, chip), o]
+            cps["1", p] = remote(s1[p], r1[p], ys.at[4 * p], yrs.at[4 * p], t1, c)
+
+    def y_step(p):
+        o = slice(PIECES[p][0], sum(PIECES[p]))
+        cps["1", p].wait_recv()
 
         def got(q, e):
-            return r1[n, pl.ds(pl.multiple_of((q * 2 + e) * rows, rows), rows), :]
-
-        s2[n, 0] = yp[rows_of(c, t2), o] + got(c, 1)
-        s2[n, 1] = yp[rows_of(1 - c, t2), o] + got(1 - c, 1)
-        cps["2", n] = remote(s2.at[n, 0], r2.at[n, 0], ys.at[4 * n + 1], yrs.at[4 * n + 1], t2, c)
-        cps["3", n] = remote(s2.at[n, 1], r2.at[n, 1], ys.at[4 * n + 2], yrs.at[4 * n + 2], t2, 1 - c)
-        sc[n] = yp[rows_of(1 - c, t), o] + got(1 - c, 0)
-        cps["4", n] = remote(sc.at[n], rc.at[n], ys.at[4 * n + 3], yrs.at[4 * n + 3], t, 1 - c)
-        yk[n] = yp[rows_of(c, t), o] + got(c, 0)
-
-    def y_done(n):
+            return r1[p][pl.ds(pl.multiple_of((q * 2 + e) * rows, rows), rows), :]
+
+        s2[p][0] = yp[rows_of(c, t2), o] + got(c, 1)
+        s2[p][1] = yp[rows_of(1 - c, t2), o] + got(1 - c, 1)
+        cps["2", p] = remote(s2[p].at[0], r2[p].at[0], ys.at[4 * p + 1], yrs.at[4 * p + 1], t2, c)
+        cps["3", p] = remote(s2[p].at[1], r2[p].at[1], ys.at[4 * p + 2], yrs.at[4 * p + 2], t2, 1 - c)
+        sc[p][...] = yp[rows_of(1 - c, t), o] + got(1 - c, 0)
+        cps["4", p] = remote(sc[p], rc[p], ys.at[4 * p + 3], yrs.at[4 * p + 3], t, 1 - c)
+        yk[p][...] = yp[rows_of(c, t), o] + got(c, 0)
+
+    def y_done(p):
         for k in "234":
-            cps[k, n].wait_recv()
-        for q, tot in ((c, yk[n] + r2[n, 0]), (1 - c, rc[n] + r2[n, 1])):
-            cols = pl.ds(pl.multiple_of(q * d_half + n * DC, DC), DC)
+            cps[k, p].wait_recv()
+        o, w = PIECES[p]
+        for q, tot in ((c, yk[p][...] + r2[p][0]), (1 - c, rc[p][...] + r2[p][1])):
+            cols = pl.ds(pl.multiple_of(q * d_half + o, 128), w)
             y_ref[:, cols] = (x_v[:, cols].astype(F32) + tot).astype(BF16)
 
     def g_part(j):
@@ -186,9 +191,9 @@
     cw[2].wait()
     for j in range(SPLIT):
         cps["h", j].wait_recv()
-    y_part(0)
-    y_part(1)
-    y_part(2)
+    y_part(0, (0,))
+    y_part(1, (1,))
+    y_part(2, (2, 3))
     for cp in sg:
         cp.wait_recv()
     g_part(0)
@@ -204,20 +209,23 @@
     dx_part(1)
     grad(3)
     y_step(2)
+    y_step(3)
     dx_part(2)
     dx_part(3)
 
     for i in range(8):
         r = ((i % 2) * 4 + i // 2) * rows
-        p_out[i] = dxp[r:r + rows, :]
+        p_out[i, :, :d_half] = dxp[r:r + rows, :]
+        p_out[i, :, d_half:] = yp[r:r + rows, FRONT:]
     for q in range(2):
-        p_out[t * 2 + q] += gc[rows_of(q, t), :].astype(F32)
+        p_out[t * 2 + q, :, :d_half] += gc[rows_of(q, t), :].astype(F32)
+        p_out[t * 2 + q, :, d_half:] += xc[rows_of(q, t), FRONT:].astype(F32)
     gc_out[...] = gc[...]
     h_out[...] = h[...]
     da_out[...] = da[...]
     db_out[...] = db[...]
-    for n in range(nd):
-        y_done(n)
+    for p in range(len(PIECES)):
+        y_done(p)
 
     for cp in sg:
         cp.wait_send()
@@ -227,10 +235,13 @@
 
 
 def _finish(y_in, p, y_ref, dx_ref):
-    d_half = p.shape[2]
-    y_ref[...] = y_in[...]
+    d_half = y_ref.shape[1] // 2
     for q in range(2):
-        dx_ref[:, q * d_half:(q + 1) * d_half] = (p[q] + p[q + 2] + p[q + 4] + p[q + 6]).astype(BF16)
+        o = q * d_half
+        tot = (p[q] + p[q + 2] + p[q + 4] + p[q + 6]).astype(BF16)
+        dx_ref[:, o:o + d_half] = tot[:, :d_half]
+        y_ref[:, o:o + FRONT] = y_in[:, o:o + FRONT]
+        y_ref[:, o + FRONT:o + d_half] = tot[:, d_half:]
 
 
 def _grads(h, da, db, xc_hbm, gc, dwd_hbm, dwg_hbm, dwu_hbm, buf_d, buf_g, xc, sem_d, sem_g, sem_x):
@@ -284,14 +295,13 @@
         S = jax.ShapeDtypeStruct
         dma = pltpu.SemaphoreType.DMA
         full = pltpu.VMEM((nf, tok, FC), F32)
-        block = pltpu.VMEM((nd, rows, DC), F32)
         y, xc, gc, h, da, db, parts = pl.pallas_call(
             _front,
             name="front",
             out_shape=(S((rows, d_full), BF16),
                        pltpu.HBM((tok, d_half), BF16), S((tok, d_half), BF16),
                        S((tok, ff), BF16), S((tok, ff), BF16), S((tok, ff), BF16))
-            + (S((8, rows, d_half), F32),),
+            + (S((8, rows, 2 * d_half - FRONT), F32),),
             in_specs=[hbm] * 5,
             out_specs=(vm, hbm, vm, vm, vm, vm, vm),
             scratch_shapes=[
@@ -301,27 +311,27 @@
                 full, full, full, full, full, full, full,
                 pltpu.VMEM((tok, ff), BF16), pltpu.VMEM((tok, ff), BF16), pltpu.VMEM((tok, ff), BF16),
                 pltpu.VMEM((tok, d_half), F32),
-                pltpu.VMEM((nd, 4 * rows, DC), F32), pltpu.VMEM((nd, 4 * rows, DC), F32),
-                pltpu.VMEM((nd, 2, rows, DC), F32), pltpu.VMEM((nd, 2, rows, DC), F32),
-                block, block, block,
+                [pltpu.VMEM((4 * rows, w), F32) for _, w in PIECES], [pltpu.VMEM((4 * rows, w), F32) for _, w in PIECES],
+                [pltpu.VMEM((2, rows, w), F32) for _, w in PIECES], [pltpu.VMEM((2, rows, w), F32) for _, w in PIECES],
+                *([pltpu.VMEM((rows, w), F32) for _, w in PIECES] for _ in range(3)),
                 pltpu.VMEM((tok, d_half), F32),
                 dma((5,)), dma((1,)), dma((7,)), dma((7,)), dma((7,)), dma((7,)),
-                dma((6 * nf,)), dma((6 * nf,)), dma((4 * nd,)), dma((4 * nd,)),
+                dma((6 * nf,)), dma((6 * nf,)), dma((4 * len(PIECES),)), dma((4 * len(PIECES),)),
             ],
             compiler_params=pltpu.CompilerParams(collective_id=0, has_side_effects=True,
                                                  vmem_limit_bytes=50 * 1024 * 1024),
         )(*(pltpu.with_memory_space_constraint(v, pltpu.HBM) for v in (x, wg, wu, wd, gy)))
         parts = lax.all_to_all(parts, ("tp", "dp"), 0, 0, tiled=True)
 
-        tr = 128
+        tr = 256
         dwd, dwg, dwu = pl.pallas_call(
             _grads,
             name="grads",
             out_shape=(S((ff, d_half), F32), S((d_half, ff), F32), S((d_half, ff), F32)),
             in_specs=[vm, vm, vm, hbm, vm],
             out_specs=(any_, any_, any_),
-            scratch_shapes=[pltpu.VMEM((16, tr, d_half), F32), pltpu.VMEM((12, tr, ff), F32),
-                            pltpu.VMEM((tok, d_half), BF16), dma((16,)), dma((12,)), dma(())],
+            scratch_shapes=[pltpu.VMEM((8, tr, d_half), F32), pltpu.VMEM((6, tr, ff), F32),
+                            pltpu.VMEM((tok, d_half), BF16), dma((8,)), dma((6,)), dma(())],
             cost_estimate=pl.CostEstimate(flops=6 * tok * d_half * ff, bytes_accessed=12 * d_half * ff,
                                           transcendentals=0),
             compiler_params=pltpu.CompilerParams(vmem_limit_bytes=34 * 1024 * 1024),

time: 44.9 us -> 44 us (0.980)
  Pallas kernels: 41.4 us -> 40.2 us
  waiting for transfers between devices: 0.01 us -> 0.54 us
    pallas_call x1, Pallas kernels: 13.7 us -> 12.7 us  [local_step(): pl.pallas_call(_grads, name='grads', out_shape=(S((ff, d_half), F32), S((...]
    all_to_all x1, waiting for transfers between devices: 0.01 us -> 0.54 us  [local_step(): parts = lax.all_to_all(parts, ('tp', 'dp'), 0, 0, tiled=True)]
  transfers between devices with their start and end apart: 1 -> 1, of which waited for: 0 -> 1; matrix products, arithmetic and copies ran while one was open for 0% -> 0% of each run, Pallas kernels for 31% -> 29%
where the time goes in v10:
time: 44 us; the launch traced here: 43.8 us
  Pallas kernels  40.2 us (91%)
  starting transfers between devices  2.4 us (5%)
  between operations  0.65 us (1%)
  waiting for transfers between devices  0.54 us (1%)
    pallas_call x1, Pallas kernels, local_step(): pl.pallas_call(_front, name='front', out_shape=(S((rows, d_full), BF16),...  26.8 us
    pallas_call x1, Pallas kernels, local_step(): pl.pallas_call(_grads, name='grads', out_shape=(S((ff, d_half), F32), S((...  12.7 us
    all_to_all x1, starting transfers between devices, local_step(): parts = lax.all_to_all(parts, ('tp', 'dp'), 0, 0, tiled=True)  2.4 us
  transfers between devices with their start and end apart: 1, of which 1 were waited for; matrix products, arithmetic and copies ran while one was open for 0% of the time, Pallas kernels for 29%

profile of v10, /device:TPU:0, one launch (start us, length us, event | category | flops | bytes accessed | tf_op | source)
XLA Modules:
  0.0 43.8 jit_solution(2194159190888233482)
XLA Ops:
  0.6 26.8 %front.1 = (bf16[16,3072]{1,0:T(8,128)(2,1)S(1)}, bf16[128,1536]{1,0:T(8,128)(2,1)}, bf16[128,1536]{1,0:T(8,128)(2,1)S(1)}, bf16[128,2048]{1,0:T(8,128)(2,1)S(1)...) custom-call(bf16[16,3072]{1,0:T(8,128)(2,1)} %x_hbm.1, ...), custom_call_target="tpu_custom_call" | custom-call | tf_op jit(solution)/shard_map/front/pallas_call | solution.py:298
  27.5 2.4 %all-to-all-start = ((f32[8,16,1664]{2,1,0:T(8,128)}), f32[8,16,1664]{2,1,0:T(8,128)S(1)}, u32[]{:S(2)}, u32[]{:S(2)}) async-start(f32[8,16,1664]{2,1,0:T(8,128)} %get-tuple-element.18), calls=%async_computation | async-start | bytes 1703936 | tf_op jit(solution)/shard_map/all_to_all | solution.py:324
  29.9 12.7 %grads.1 = (f32[2048,1536]{1,0:T(8,128)}, f32[1536,2048]{1,0:T(8,128)}, f32[1536,2048]{1,0:T(8,128)}) custom-call(bf16[128,2048]{1,0:T(8,128)(2,1)S(1)} %get-tuple-element.21.h, bf16[128,2048]{1,0:T(8,128)(2,1)S(1)} %get-tuple-element.22.da, bf16[128,2048]{1,0:T(8,128)(2,1)S(1)} %get-tuple-element.23.db, bf16[128,1536]{1,0:T(8,128)(2,1)} %get-tuple-element.24.xc_hbm, ...), custom_call_target="tpu_custom_call" | custom-call | flops 2415919104 | bytes 37748736 | tf_op jit(solution)/shard_map/grads/pallas_call | solution.py:327
  42.6 0.5 %all-to-all-done.p = f32[8,16,1664]{2,1,0:T(8,128)S(1)} async-done(((f32[8,16,1664]{2,1,0:T(8,128)}), f32[8,16,1664]{2,1,0:T(8,128)S(1)}, u32[]{:S(2)}, u32[]{:S(2)}) %all-to-all-start) | async-done | bytes 852000 | tf_op jit(solution)/shard_map/all_to_all | solution.py:324
  43.1 0.7 %finish.1 = (bf16[16,3072]{1,0:T(8,128)(2,1)}, bf16[16,3072]{1,0:T(8,128)(2,1)}) custom-call(bf16[16,3072]{1,0:T(8,128)(2,1)S(1)} %get-tuple-element.17.y_in, f32[8,16,1664]{2,1,0:T(8,128)S(1)} %all-to-all-done.p), custom_call_target="tpu_custom_call" | custom-call | tf_op jit(solution)/shard_map/finish/pallas_call | solution.py:339
Async XLA Ops:
  27.5 15.6 %all-to-all-start = ((f32[8,16,1664]{2,1,0:T(8,128)}), f32[8,16,1664]{2,1,0:T(8,128)S(1)}, u32[]{:S(2)}, u32[]{:S(2)}) async-start(f32[8,16,1664]{2,1,0:T(8,128)} %get-tuple-element.18), calls=%async_computation | async-start | bytes 1703936 | tf_op jit(solution)/shard_map/all_to_all | solution.py:324

commit v11 on v10

--- a/solution.py
+++ b/solution.py
@@ -23,9 +23,9 @@
 
 
 def _front(x_hbm, wg_hbm, wu_hbm, wd_hbm, gy_hbm,
-           y_ref, xc_out, gc_out, h_out, da_out, db_out, p_out,
-           x_v, gy_v, wg, wu, wd, xc, gc,
-           pa, pb, pg, ra, rb, rg, sd, h, da, db,
+           y_ref, xc_out, gc, h, da, db, p_out,
+           x_v, gy_v, wg, wu, wd, xc,
+           pa, pb, pg, ra, rb, rg, sd,
            yp, s1, r1, s2, r2, sc, rc, yk, dxp,
            w_sem, o_sem, xs, xrs, gs, grs, es, ers, ys, yrs):
     rows, d_full = x_v.shape
@@ -220,10 +220,6 @@
     for q in range(2):
         p_out[t * 2 + q, :, :d_half] += gc[rows_of(q, t), :].astype(F32)
         p_out[t * 2 + q, :, d_half:] += xc[rows_of(q, t), FRONT:].astype(F32)
-    gc_out[...] = gc[...]
-    h_out[...] = h[...]
-    da_out[...] = da[...]
-    db_out[...] = db[...]
     for p in range(len(PIECES)):
         y_done(p)
 
@@ -307,9 +303,8 @@
             scratch_shapes=[
                 pltpu.VMEM((rows, d_full), BF16), pltpu.VMEM((rows, d_full), BF16),
                 pltpu.VMEM((d_half, ff), BF16), pltpu.VMEM((d_half, ff), BF16), pltpu.VMEM((ff, d_half), BF16),
-                pltpu.VMEM((tok, d_half), BF16), pltpu.VMEM((tok, d_half), BF16),
+                pltpu.VMEM((tok, d_half), BF16),
                 full, full, full, full, full, full, full,
-                pltpu.VMEM((tok, ff), BF16), pltpu.VMEM((tok, ff), BF16), pltpu.VMEM((tok, ff), BF16),
                 pltpu.VMEM((tok, d_half), F32),
                 [pltpu.VMEM((4 * rows, w), F32) for _, w in PIECES], [pltpu.VMEM((4 * rows, w), F32) for _, w in PIECES],
                 [pltpu.VMEM((2, rows, w), F32) for _, w in PIECES], [pltpu.VMEM((2, rows, w), F32) for _, w in PIECES],

time: 44 us -> 44 us (level)
  no operation moved by 1% of the time
where the time goes in v11:
time: 44 us; the launch traced here: 43.8 us
  Pallas kernels  40.1 us (91%)
  starting transfers between devices  2.55 us (6%)
  between operations  0.65 us (1%)
  waiting for transfers between devices  0.54 us (1%)
    pallas_call x1, Pallas kernels, local_step(): pl.pallas_call(_front, name='front', out_shape=(S((rows, d_full), BF16),...  26.7 us
    pallas_call x1, Pallas kernels, local_step(): pl.pallas_call(_grads, name='grads', out_shape=(S((ff, d_half), F32), S((...  12.7 us
    all_to_all x1, starting transfers between devices, local_step(): parts = lax.all_to_all(parts, ('tp', 'dp'), 0, 0, tiled=True)  2.55 us
  transfers between devices with their start and end apart: 1, of which 1 were waited for; matrix products, arithmetic and copies ran while one was open for 0% of the time, Pallas kernels for 29%

profile of v11, /device:TPU:0, one launch (start us, length us, event | category | flops | bytes accessed | tf_op | source)
XLA Modules:
  0.0 43.8 jit_solution(7094133889496361405)
XLA Ops:
  0.6 26.7 %front.1 = (bf16[16,3072]{1,0:T(8,128)(2,1)S(1)}, bf16[128,1536]{1,0:T(8,128)(2,1)}, bf16[128,1536]{1,0:T(8,128)(2,1)S(1)}, bf16[128,2048]{1,0:T(8,128)(2,1)S(1)...) custom-call(bf16[16,3072]{1,0:T(8,128)(2,1)} %x_hbm.1, ...), custom_call_target="tpu_custom_call" | custom-call | tf_op jit(solution)/shard_map/front/pallas_call | solution.py:294
  27.3 2.6 %all-to-all-start = ((f32[8,16,1664]{2,1,0:T(8,128)}), f32[8,16,1664]{2,1,0:T(8,128)S(1)}, u32[]{:S(2)}, u32[]{:S(2)}) async-start(f32[8,16,1664]{2,1,0:T(8,128)} %get-tuple-element.18), calls=%async_computation | async-start | bytes 1703936 | tf_op jit(solution)/shard_map/all_to_all | solution.py:319
  29.9 12.7 %grads.1 = (f32[2048,1536]{1,0:T(8,128)}, f32[1536,2048]{1,0:T(8,128)}, f32[1536,2048]{1,0:T(8,128)}) custom-call(bf16[128,2048]{1,0:T(8,128)(2,1)S(1)} %get-tuple-element.21.h, bf16[128,2048]{1,0:T(8,128)(2,1)S(1)} %get-tuple-element.22.da, bf16[128,2048]{1,0:T(8,128)(2,1)S(1)} %get-tuple-element.23.db, bf16[128,1536]{1,0:T(8,128)(2,1)} %get-tuple-element.24.xc_hbm, ...), custom_call_target="tpu_custom_call" | custom-call | flops 2415919104 | bytes 37748736 | tf_op jit(solution)/shard_map/grads/pallas_call | solution.py:322
  42.6 0.5 %all-to-all-done.p = f32[8,16,1664]{2,1,0:T(8,128)S(1)} async-done(((f32[8,16,1664]{2,1,0:T(8,128)}), f32[8,16,1664]{2,1,0:T(8,128)S(1)}, u32[]{:S(2)}, u32[]{:S(2)}) %all-to-all-start) | async-done | bytes 852000 | tf_op jit(solution)/shard_map/all_to_all | solution.py:319
  43.1 0.7 %finish.1 = (bf16[16,3072]{1,0:T(8,128)(2,1)}, bf16[16,3072]{1,0:T(8,128)(2,1)}) custom-call(bf16[16,3072]{1,0:T(8,128)(2,1)S(1)} %get-tuple-element.17.y_in, f32[8,16,1664]{2,1,0:T(8,128)S(1)} %all-to-all-done.p), custom_call_target="tpu_custom_call" | custom-call | tf_op jit(solution)/shard_map/finish/pallas_call | solution.py:334
Async XLA Ops:
  27.3 15.8 %all-to-all-start = ((f32[8,16,1664]{2,1,0:T(8,128)}), f32[8,16,1664]{2,1,0:T(8,128)S(1)}, u32[]{:S(2)}, u32[]{:S(2)}) async-start(f32[8,16,1664]{2,1,0:T(8,128)} %get-tuple-element.18), calls=%async_computation | async-start | bytes 1703936 | tf_op jit(solution)/shard_map/all_to_all | solution.py:319

commit v12 on v11

--- a/solution.py
+++ b/solution.py
@@ -206,10 +206,10 @@
     dx_part(0)
     grad(2)
     y_step(1)
-    dx_part(1)
     grad(3)
     y_step(2)
     y_step(3)
+    dx_part(1)
     dx_part(2)
     dx_part(3)
 

time: 44 us -> 44.7 us (1.016)
  Pallas kernels: 40.1 us -> 41.1 us
    pallas_call x1, Pallas kernels: 26.7 us -> 27.7 us  [local_step(): pl.pallas_call(_front, name='front', out_shape=(S((rows, d_full), BF16),...]
where the time goes in v12:
time: 44.7 us; the launch traced here: 44.5 us
  Pallas kernels  41.1 us (92%)
  starting transfers between devices  2.3 us (5%)
  between operations  0.66 us (1%)
  waiting for transfers between devices  0.47 us (1%)
    pallas_call x1, Pallas kernels, local_step(): pl.pallas_call(_front, name='front', out_shape=(S((rows, d_full), BF16),...  27.7 us
    pallas_call x1, Pallas kernels, local_step(): pl.pallas_call(_grads, name='grads', out_shape=(S((ff, d_half), F32), S((...  12.7 us
    all_to_all x1, starting transfers between devices, local_step(): parts = lax.all_to_all(parts, ('tp', 'dp'), 0, 0, tiled=True)  2.3 us
  transfers between devices with their start and end apart: 1, of which 1 were waited for; matrix products, arithmetic and copies ran while one was open for 0% of the time, Pallas kernels for 29%

profile of v12, /device:TPU:0, one launch (start us, length us, event | category | flops | bytes accessed | tf_op | source)
XLA Modules:
  0.0 44.5 jit_solution(4911920066784919258)
XLA Ops:
  0.6 27.7 %front.1 = (bf16[16,3072]{1,0:T(8,128)(2,1)S(1)}, bf16[128,1536]{1,0:T(8,128)(2,1)}, bf16[128,1536]{1,0:T(8,128)(2,1)S(1)}, bf16[128,2048]{1,0:T(8,128)(2,1)S(1)...) custom-call(bf16[16,3072]{1,0:T(8,128)(2,1)} %x_hbm.1, ...), custom_call_target="tpu_custom_call" | custom-call | tf_op jit(solution)/shard_map/front/pallas_call | solution.py:294
  28.3 2.3 %all-to-all-start = ((f32[8,16,1664]{2,1,0:T(8,128)}), f32[8,16,1664]{2,1,0:T(8,128)S(1)}, u32[]{:S(2)}, u32[]{:S(2)}) async-start(f32[8,16,1664]{2,1,0:T(8,128)} %get-tuple-element.18), calls=%async_computation | async-start | bytes 1703936 | tf_op jit(solution)/shard_map/all_to_all | solution.py:319
  30.7 12.7 %grads.1 = (f32[2048,1536]{1,0:T(8,128)}, f32[1536,2048]{1,0:T(8,128)}, f32[1536,2048]{1,0:T(8,128)}) custom-call(bf16[128,2048]{1,0:T(8,128)(2,1)S(1)} %get-tuple-element.21.h, bf16[128,2048]{1,0:T(8,128)(2,1)S(1)} %get-tuple-element.22.da, bf16[128,2048]{1,0:T(8,128)(2,1)S(1)} %get-tuple-element.23.db, bf16[128,1536]{1,0:T(8,128)(2,1)} %get-tuple-element.24.xc_hbm, ...), custom_call_target="tpu_custom_call" | custom-call | flops 2415919104 | bytes 37748736 | tf_op jit(solution)/shard_map/grads/pallas_call | solution.py:322
  43.4 0.5 %all-to-all-done.p = f32[8,16,1664]{2,1,0:T(8,128)S(1)} async-done(((f32[8,16,1664]{2,1,0:T(8,128)}), f32[8,16,1664]{2,1,0:T(8,128)S(1)}, u32[]{:S(2)}, u32[]{:S(2)}) %all-to-all-start) | async-done | bytes 852000 | tf_op jit(solution)/shard_map/all_to_all | solution.py:319
  43.8 0.7 %finish.1 = (bf16[16,3072]{1,0:T(8,128)(2,1)}, bf16[16,3072]{1,0:T(8,128)(2,1)}) custom-call(bf16[16,3072]{1,0:T(8,128)(2,1)S(1)} %get-tuple-element.17.y_in, f32[8,16,1664]{2,1,0:T(8,128)S(1)} %all-to-all-done.p), custom_call_target="tpu_custom_call" | custom-call | tf_op jit(solution)/shard_map/finish/pallas_call | solution.py:334
Async XLA Ops:
  28.3 15.5 %all-to-all-start = ((f32[8,16,1664]{2,1,0:T(8,128)}), f32[8,16,1664]{2,1,0:T(8,128)S(1)}, u32[]{:S(2)}, u32[]{:S(2)}) async-start(f32[8,16,1664]{2,1,0:T(8,128)} %get-tuple-element.18), calls=%async_computation | async-start | bytes 1703936 | tf_op jit(solution)/shard_map/all_to_all | solution.py:319

commit v13 on v11

--- a/solution.py
+++ b/solution.py
@@ -16,8 +16,8 @@
 
 FC = 512
 DC = 512
-PIECES = ((0, 512), (512, 512), (1024, 256), (1280, 128))
-FRONT = 1408
+PIECES = ((0, 512), (512, 512), (1024, 256), (1280, 256))
+FRONT = 1536
 SPLIT = 2
 RB = 32
 
@@ -216,10 +216,12 @@
     for i in range(8):
         r = ((i % 2) * 4 + i // 2) * rows
         p_out[i, :, :d_half] = dxp[r:r + rows, :]
-        p_out[i, :, d_half:] = yp[r:r + rows, FRONT:]
+        if FRONT < d_half:
+            p_out[i, :, d_half:] = yp[r:r + rows, FRONT:]
     for q in range(2):
         p_out[t * 2 + q, :, :d_half] += gc[rows_of(q, t), :].astype(F32)
-        p_out[t * 2 + q, :, d_half:] += xc[rows_of(q, t), FRONT:].astype(F32)
+        if FRONT < d_half:
+            p_out[t * 2 + q, :, d_half:] += xc[rows_of(q, t), FRONT:].astype(F32)
     for p in range(len(PIECES)):
         y_done(p)
 
@@ -237,7 +239,8 @@
         tot = (p[q] + p[q + 2] + p[q + 4] + p[q + 6]).astype(BF16)
         dx_ref[:, o:o + d_half] = tot[:, :d_half]
         y_ref[:, o:o + FRONT] = y_in[:, o:o + FRONT]
-        y_ref[:, o + FRONT:o + d_half] = tot[:, d_half:]
+        if FRONT < d_half:
+            y_ref[:, o + FRONT:o + d_half] = tot[:, d_half:]
 
 
 def _grads(h, da, db, xc_hbm, gc, dwd_hbm, dwg_hbm, dwu_hbm, buf_d, buf_g, xc, sem_d, sem_g, sem_x):

time: 44 us -> 43.9 us (level)
  waiting for transfers between devices: 0.54 us -> 0.01 us
    all_to_all x1, waiting for transfers between devices: 0.54 us -> 0.01 us  [local_step(): parts = lax.all_to_all(parts, ('tp', 'dp'), 0, 0, tiled=True)]
  transfers between devices with their start and end apart: 1 -> 1, of which waited for: 1 -> 0; matrix products, arithmetic and copies ran while one was open for 0% -> 0% of each run, Pallas kernels for 29% -> 29%
where the time goes in v13:
time: 43.9 us; the launch traced here: 43.7 us
  Pallas kernels  40.4 us (92%)
  starting transfers between devices  2.62 us (6%)
  between operations  0.66 us (2%)
    pallas_call x1, Pallas kernels, local_step(): pl.pallas_call(_front, name='front', out_shape=(S((rows, d_full), BF16),...  27 us
    pallas_call x1, Pallas kernels, local_step(): pl.pallas_call(_grads, name='grads', out_shape=(S((ff, d_half), F32), S((...  12.7 us
    all_to_all x1, starting transfers between devices, local_step(): parts = lax.all_to_all(parts, ('tp', 'dp'), 0, 0, tiled=True)  2.62 us
  transfers between devices with their start and end apart: 1, of which 0 were waited for; matrix products, arithmetic and copies ran while one was open for 0% of the time, Pallas kernels for 29%

profile of v13, /device:TPU:0, one launch (start us, length us, event | category | flops | bytes accessed | tf_op | source)
XLA Modules:
  0.0 43.7 jit_solution(14907519366207042255)
XLA Ops:
  0.6 27.0 %front.1 = (bf16[16,3072]{1,0:T(8,128)(2,1)S(1)}, bf16[128,1536]{1,0:T(8,128)(2,1)}, bf16[128,1536]{1,0:T(8,128)(2,1)S(1)}, bf16[128,2048]{1,0:T(8,128)(2,1)S(1)...) custom-call(bf16[16,3072]{1,0:T(8,128)(2,1)} %x_hbm.1, ...), custom_call_target="tpu_custom_call" | custom-call | tf_op jit(solution)/shard_map/front/pallas_call | solution.py:297
  27.7 2.6 %all-to-all-start = ((f32[8,16,1536]{2,1,0:T(8,128)}), f32[8,16,1536]{2,1,0:T(8,128)S(1)}, u32[]{:S(2)}, u32[]{:S(2)}) async-start(f32[8,16,1536]{2,1,0:T(8,128)} %get-tuple-element.18), calls=%async_computation | async-start | bytes 1572864 | tf_op jit(solution)/shard_map/all_to_all | solution.py:322
  30.3 12.7 %grads.1 = (f32[2048,1536]{1,0:T(8,128)}, f32[1536,2048]{1,0:T(8,128)}, f32[1536,2048]{1,0:T(8,128)}) custom-call(bf16[128,2048]{1,0:T(8,128)(2,1)S(1)} %get-tuple-element.21.h, bf16[128,2048]{1,0:T(8,128)(2,1)S(1)} %get-tuple-element.22.da, bf16[128,2048]{1,0:T(8,128)(2,1)S(1)} %get-tuple-element.23.db, bf16[128,1536]{1,0:T(8,128)(2,1)} %get-tuple-element.24.xc_hbm, ...), custom_call_target="tpu_custom_call" | custom-call | flops 2415919104 | bytes 37748736 | tf_op jit(solution)/shard_map/grads/pallas_call | solution.py:325
  43.0 0.0 all-to-all-done.p
  43.0 0.7 %finish.1 = (bf16[16,3072]{1,0:T(8,128)(2,1)}, bf16[16,3072]{1,0:T(8,128)(2,1)}) custom-call(bf16[16,3072]{1,0:T(8,128)(2,1)S(1)} %get-tuple-element.17.y_in, f32[8,16,1536]{2,1,0:T(8,128)S(1)} %all-to-all-done.p), custom_call_target="tpu_custom_call" | custom-call | tf_op jit(solution)/shard_map/finish/pallas_call | solution.py:337
Async XLA Ops:
  27.7 15.3 %all-to-all-start = ((f32[8,16,1536]{2,1,0:T(8,128)}), f32[8,16,1536]{2,1,0:T(8,128)S(1)}, u32[]{:S(2)}, u32[]{:S(2)}) async-start(f32[8,16,1536]{2,1,0:T(8,128)} %get-tuple-element.18), calls=%async_computation | async-start | bytes 1572864 | tf_op jit(solution)/shard_map/all_to_all | solution.py:322

commit v14 on v13

--- a/solution.py
+++ b/solution.py
@@ -16,9 +16,9 @@
 
 FC = 512
 DC = 512
-PIECES = ((0, 512), (512, 512), (1024, 256), (1280, 256))
+PIECES = ((0, 512), (512, 512), (1024, 384), (1408, 128))
 FRONT = 1536
-SPLIT = 2
+SPLIT = 1
 RB = 32
 
 

time: 43.9 us -> 43.9 us (level)
  no operation moved by 1% of the time
where the time goes in v14:
time: 43.9 us; the launch traced here: 43.7 us
  Pallas kernels  40.4 us (92%)
  starting transfers between devices  2.69 us (6%)
  between operations  0.66 us (2%)
    pallas_call x1, Pallas kernels, local_step(): pl.pallas_call(_front, name='front', out_shape=(S((rows, d_full), BF16),...  27 us
    pallas_call x1, Pallas kernels, local_step(): pl.pallas_call(_grads, name='grads', out_shape=(S((ff, d_half), F32), S((...  12.7 us
    all_to_all x1, starting transfers between devices, local_step(): parts = lax.all_to_all(parts, ('tp', 'dp'), 0, 0, tiled=True)  2.69 us
  transfers between devices with their start and end apart: 1, of which 0 were waited for; matrix products, arithmetic and copies ran while one was open for 0% of the time, Pallas kernels for 29%

profile of v14, /device:TPU:0, one launch (start us, length us, event | category | flops | bytes accessed | tf_op | source)
XLA Modules:
  0.0 43.7 jit_solution(4317996774432540610)
XLA Ops:
  0.6 27.0 %front.1 = (bf16[16,3072]{1,0:T(8,128)(2,1)S(1)}, bf16[128,1536]{1,0:T(8,128)(2,1)}, bf16[128,1536]{1,0:T(8,128)(2,1)S(1)}, bf16[128,2048]{1,0:T(8,128)(2,1)S(1)...) custom-call(bf16[16,3072]{1,0:T(8,128)(2,1)} %x_hbm.1, ...), custom_call_target="tpu_custom_call" | custom-call | tf_op jit(solution)/shard_map/front/pallas_call | solution.py:297
  27.6 2.7 %all-to-all-start = ((f32[8,16,1536]{2,1,0:T(8,128)}), f32[8,16,1536]{2,1,0:T(8,128)S(1)}, u32[]{:S(2)}, u32[]{:S(2)}) async-start(f32[8,16,1536]{2,1,0:T(8,128)} %get-tuple-element.18), calls=%async_computation | async-start | bytes 1572864 | tf_op jit(solution)/shard_map/all_to_all | solution.py:322
  30.3 12.7 %grads.1 = (f32[2048,1536]{1,0:T(8,128)}, f32[1536,2048]{1,0:T(8,128)}, f32[1536,2048]{1,0:T(8,128)}) custom-call(bf16[128,2048]{1,0:T(8,128)(2,1)S(1)} %get-tuple-element.21.h, bf16[128,2048]{1,0:T(8,128)(2,1)S(1)} %get-tuple-element.22.da, bf16[128,2048]{1,0:T(8,128)(2,1)S(1)} %get-tuple-element.23.db, bf16[128,1536]{1,0:T(8,128)(2,1)} %get-tuple-element.24.xc_hbm, ...), custom_call_target="tpu_custom_call" | custom-call | flops 2415919104 | bytes 37748736 | tf_op jit(solution)/shard_map/grads/pallas_call | solution.py:325
  43.0 0.0 all-to-all-done.p
  43.0 0.7 %finish.1 = (bf16[16,3072]{1,0:T(8,128)(2,1)}, bf16[16,3072]{1,0:T(8,128)(2,1)}) custom-call(bf16[16,3072]{1,0:T(8,128)(2,1)S(1)} %get-tuple-element.17.y_in, f32[8,16,1536]{2,1,0:T(8,128)S(1)} %all-to-all-done.p), custom_call_target="tpu_custom_call" | custom-call | tf_op jit(solution)/shard_map/finish/pallas_call | solution.py:337
Async XLA Ops:
  27.6 15.4 %all-to-all-start = ((f32[8,16,1536]{2,1,0:T(8,128)}), f32[8,16,1536]{2,1,0:T(8,128)S(1)}, u32[]{:S(2)}, u32[]{:S(2)}) async-start(f32[8,16,1536]{2,1,0:T(8,128)} %get-tuple-element.18), calls=%async_computation | async-start | bytes 1572864 | tf_op jit(solution)/shard_map/all_to_all | solution.py:322

commit v15 on v13

--- a/solution.py
+++ b/solution.py
@@ -232,24 +232,21 @@
     out_x.wait()
 
 
-def _finish(y_in, p, y_ref, dx_ref):
-    d_half = y_ref.shape[1] // 2
+def _finish(p, dx_ref):
+    d_half = p.shape[2]
     for q in range(2):
-        o = q * d_half
-        tot = (p[q] + p[q + 2] + p[q + 4] + p[q + 6]).astype(BF16)
-        dx_ref[:, o:o + d_half] = tot[:, :d_half]
-        y_ref[:, o:o + FRONT] = y_in[:, o:o + FRONT]
-        if FRONT < d_half:
-            y_ref[:, o + FRONT:o + d_half] = tot[:, d_half:]
-
-
-def _grads(h, da, db, xc_hbm, gc, dwd_hbm, dwg_hbm, dwu_hbm, buf_d, buf_g, xc, sem_d, sem_g, sem_x):
+        dx_ref[:, q * d_half:(q + 1) * d_half] = (p[q] + p[q + 2] + p[q + 4] + p[q + 6]).astype(BF16)
+
+
+def _grads(h, da, db, xc_hbm, gc, y, dwd_hbm, dwg_hbm, dwu_hbm, y_hbm, buf_d, buf_g, xc, sem_d, sem_g, sem_x, sem_y):
     ff = h.shape[1]
     d_half = xc.shape[1]
     nb_d, tr_d = buf_d.shape[:2]
     nb_g, tr_g = buf_g.shape[:2]
     cx = pltpu.make_async_copy(xc_hbm, xc, sem_x)
     cx.start()
+    cy = pltpu.make_async_copy(y, y_hbm, sem_y)
+    cy.start()
 
     def run(lhs, rhs, out, buf, sem, n, tr, nb, start, prev_out):
         def step(i, carry):
@@ -279,6 +276,7 @@
         pltpu.make_async_copy(buf_d.at[s], dwd_hbm.at[pl.ds(0, tr_d), :], sem_d.at[s]).wait()
     for s in range(nb_g):
         pltpu.make_async_copy(buf_g.at[s], dwu_hbm.at[pl.ds(0, tr_g), :], sem_g.at[s]).wait()
+    cy.wait()
 
 
 def solution(mesh):
@@ -322,26 +320,26 @@
         parts = lax.all_to_all(parts, ("tp", "dp"), 0, 0, tiled=True)
 
         tr = 256
-        dwd, dwg, dwu = pl.pallas_call(
+        dwd, dwg, dwu, y = pl.pallas_call(
             _grads,
             name="grads",
-            out_shape=(S((ff, d_half), F32), S((d_half, ff), F32), S((d_half, ff), F32)),
-            in_specs=[vm, vm, vm, hbm, vm],
-            out_specs=(any_, any_, any_),
+            out_shape=(S((ff, d_half), F32), S((d_half, ff), F32), S((d_half, ff), F32), S((rows, d_full), BF16)),
+            in_specs=[vm, vm, vm, hbm, vm, vm],
+            out_specs=(any_, any_, any_, hbm),
             scratch_shapes=[pltpu.VMEM((8, tr, d_half), F32), pltpu.VMEM((6, tr, ff), F32),
-                            pltpu.VMEM((tok, d_half), BF16), dma((8,)), dma((6,)), dma(())],
+                            pltpu.VMEM((tok, d_half), BF16), dma((8,)), dma((6,)), dma(()), dma(())],
             cost_estimate=pl.CostEstimate(flops=6 * tok * d_half * ff, bytes_accessed=12 * d_half * ff,
                                           transcendentals=0),
             compiler_params=pltpu.CompilerParams(vmem_limit_bytes=34 * 1024 * 1024),
-        )(h, da, db, pltpu.with_memory_space_constraint(xc, pltpu.HBM), gc)
-        y, dx = pl.pallas_call(
+        )(h, da, db, pltpu.with_memory_space_constraint(xc, pltpu.HBM), gc, y)
+        dx = pl.pallas_call(
             _finish,
             name="finish",
-            out_shape=(S((rows, d_full), BF16), S((rows, d_full), BF16)),
-            in_specs=[vm] * 2,
-            out_specs=(vm, vm),
+            out_shape=S((rows, d_full), BF16),
+            in_specs=[vm],
+            out_specs=vm,
             compiler_params=pltpu.CompilerParams(vmem_limit_bytes=6 * 1024 * 1024),
-        )(y, parts)
+        )(parts)
         return y, dx, dwg, dwu, dwd
 
     row_spec = P(("dp", "tp"), None)

time: 43.9 us -> 43.8 us (level)
  no operation moved by 1% of the time
where the time goes in v15:
time: 43.8 us; the launch traced here: 43.7 us
  Pallas kernels  40.4 us (92%)
  starting transfers between devices  2.62 us (6%)
  between operations  0.66 us (2%)
    pallas_call x1, Pallas kernels, local_step(): pl.pallas_call(_front, name='front', out_shape=(S((rows, d_full), BF16),...  27 us
    pallas_call x1, Pallas kernels, local_step(): pl.pallas_call(_grads, name='grads', out_shape=(S((ff, d_half), F32), S((...  12.7 us
    all_to_all x1, starting transfers between devices, local_step(): parts = lax.all_to_all(parts, ('tp', 'dp'), 0, 0, tiled=True)  2.62 us
  transfers between devices with their start and end apart: 1, of which 0 were waited for; matrix products, arithmetic and copies ran while one was open for 0% of the time, Pallas kernels for 29%

profile of v15, /device:TPU:0, one launch (start us, length us, event | category | flops | bytes accessed | tf_op | source)
XLA Modules:
  0.0 43.7 jit_solution(16646383753691163551)
XLA Ops:
  0.6 27.0 %front.1 = (bf16[16,3072]{1,0:T(8,128)(2,1)S(1)}, bf16[128,1536]{1,0:T(8,128)(2,1)}, bf16[128,1536]{1,0:T(8,128)(2,1)S(1)}, bf16[128,2048]{1,0:T(8,128)(2,1)S(1)...) custom-call(bf16[16,3072]{1,0:T(8,128)(2,1)} %x_hbm.1, ...), custom_call_target="tpu_custom_call" | custom-call | tf_op jit(solution)/shard_map/front/pallas_call | solution.py:295
  27.7 2.6 %all-to-all-start = ((f32[8,16,1536]{2,1,0:T(8,128)}), f32[8,16,1536]{2,1,0:T(8,128)S(1)}, u32[]{:S(2)}, u32[]{:S(2)}) async-start(f32[8,16,1536]{2,1,0:T(8,128)} %get-tuple-element.23), calls=%async_computation | async-start | bytes 1572864 | tf_op jit(solution)/shard_map/all_to_all | solution.py:320
  30.3 12.7 %grads.1 = (f32[2048,1536]{1,0:T(8,128)}, f32[1536,2048]{1,0:T(8,128)}, f32[1536,2048]{1,0:T(8,128)}, bf16[16,3072]{1,0:T(8,128)(2,1)}) custom-call(bf16[128,2048]{1,0:T(8,128)(2,1)S(1)} %get-tuple-element.16.h, bf16[128,2048]{1,0:T(8,128)(2,1)S(1)} %get-tuple-element.17.da, bf16[128,2048]{1,0:T(8,128)(2,1)S(1)} %get-tuple-element.18.db, ...), custom_call_target="tpu_custom_call" | custom-call | flops 2415919104 | bytes 37748736 | tf_op jit(solution)/shard_map/grads/pallas_call | solution.py:323
  43.0 0.0 all-to-all-done.p
  43.0 0.7 %finish.1 = bf16[16,3072]{1,0:T(8,128)(2,1)} custom-call(f32[8,16,1536]{2,1,0:T(8,128)S(1)} %all-to-all-done.p), custom_call_target="tpu_custom_call" | custom-call | tf_op jit(solution)/shard_map/finish/pallas_call | solution.py:335
Async XLA Ops:
  27.7 15.3 %all-to-all-start = ((f32[8,16,1536]{2,1,0:T(8,128)}), f32[8,16,1536]{2,1,0:T(8,128)S(1)}, u32[]{:S(2)}, u32[]{:S(2)}) async-start(f32[8,16,1536]{2,1,0:T(8,128)} %get-tuple-element.23), calls=%async_computation | async-start | bytes 1572864 | tf_op jit(solution)/shard_map/all_to_all | solution.py:320

commit v16 on v15

--- a/solution.py
+++ b/solution.py
@@ -248,7 +248,7 @@
     cy = pltpu.make_async_copy(y, y_hbm, sem_y)
     cy.start()
 
-    def run(lhs, rhs, out, buf, sem, n, tr, nb, start, prev_out):
+    def run(lhs, rhs, out, buf, sem, n, tr, nb, start, prev_out, first=0):
         def step(i, carry):
             slot = lax.rem(i + start, nb)
             r = pl.multiple_of(i * tr, tr)
@@ -264,11 +264,15 @@
             pltpu.make_async_copy(buf.at[slot], out.at[pl.ds(r, tr), :], sem.at[slot]).start()
             return carry
 
-        lax.fori_loop(0, n, step, 0)
+        lax.fori_loop(first, n, step, 0)
 
     n_d = ff // tr_d
     n_g = d_half // tr_g
-    run(h, gc, dwd_hbm, buf_d, sem_d, n_d, tr_d, nb_d, 0, dwd_hbm)
+    for r in range(0, tr_d, tr_d // 2):
+        i = pl.ds(r, tr_d // 2)
+        buf_d[0, i, :] = lax.dot_general(h[:, i], gc[...], TN, preferred_element_type=F32)
+        pltpu.make_async_copy(buf_d.at[0, i, :], dwd_hbm.at[i, :], sem_d.at[0]).start()
+    run(h, gc, dwd_hbm, buf_d, sem_d, n_d, tr_d, nb_d, 0, dwd_hbm, 1)
     cx.wait()
     run(xc, da, dwg_hbm, buf_g, sem_g, n_g, tr_g, nb_g, 0, dwg_hbm)
     run(xc, db, dwu_hbm, buf_g, sem_g, n_g, tr_g, nb_g, n_g, dwu_hbm)

time: 43.8 us -> 43.7 us (level)
  no operation moved by 1% of the time
where the time goes in v16:
time: 43.7 us; the launch traced here: 43.6 us
  Pallas kernels  40.3 us (92%)
  starting transfers between devices  2.62 us (6%)
  between operations  0.66 us (2%)
    pallas_call x1, Pallas kernels, local_step(): pl.pallas_call(_front, name='front', out_shape=(S((rows, d_full), BF16),...  27 us
    pallas_call x1, Pallas kernels, local_step(): pl.pallas_call(_grads, name='grads', out_shape=(S((ff, d_half), F32), S((...  12.6 us
    all_to_all x1, starting transfers between devices, local_step(): parts = lax.all_to_all(parts, ('tp', 'dp'), 0, 0, tiled=True)  2.62 us
  transfers between devices with their start and end apart: 1, of which 0 were waited for; matrix products, arithmetic and copies ran while one was open for 0% of the time, Pallas kernels for 29%

profile of v16, /device:TPU:0, one launch (start us, length us, event | category | flops | bytes accessed | tf_op | source)
XLA Modules:
  0.0 43.6 jit_solution(4466284428193347665)
XLA Ops:
  0.6 27.0 %front.1 = (bf16[16,3072]{1,0:T(8,128)(2,1)S(1)}, bf16[128,1536]{1,0:T(8,128)(2,1)}, bf16[128,1536]{1,0:T(8,128)(2,1)S(1)}, bf16[128,2048]{1,0:T(8,128)(2,1)S(1)...) custom-call(bf16[16,3072]{1,0:T(8,128)(2,1)} %x_hbm.1, ...), custom_call_target="tpu_custom_call" | custom-call | tf_op jit(solution)/shard_map/front/pallas_call | solution.py:299
  27.7 2.6 %all-to-all-start = ((f32[8,16,1536]{2,1,0:T(8,128)}), f32[8,16,1536]{2,1,0:T(8,128)S(1)}, u32[]{:S(2)}, u32[]{:S(2)}) async-start(f32[8,16,1536]{2,1,0:T(8,128)} %get-tuple-element.23), calls=%async_computation | async-start | bytes 1572864 | tf_op jit(solution)/shard_map/all_to_all | solution.py:324
  30.3 12.6 %grads.1 = (f32[2048,1536]{1,0:T(8,128)}, f32[1536,2048]{1,0:T(8,128)}, f32[1536,2048]{1,0:T(8,128)}, bf16[16,3072]{1,0:T(8,128)(2,1)}) custom-call(bf16[128,2048]{1,0:T(8,128)(2,1)S(1)} %get-tuple-element.16.h, bf16[128,2048]{1,0:T(8,128)(2,1)S(1)} %get-tuple-element.17.da, bf16[128,2048]{1,0:T(8,128)(2,1)S(1)} %get-tuple-element.18.db, ...), custom_call_target="tpu_custom_call" | custom-call | flops 2415919104 | bytes 37748736 | tf_op jit(solution)/shard_map/grads/pallas_call | solution.py:327
  42.9 0.0 all-to-all-done.p
  42.9 0.7 %finish.1 = bf16[16,3072]{1,0:T(8,128)(2,1)} custom-call(f32[8,16,1536]{2,1,0:T(8,128)S(1)} %all-to-all-done.p), custom_call_target="tpu_custom_call" | custom-call | tf_op jit(solution)/shard_map/finish/pallas_call | solution.py:339
Async XLA Ops:
  27.7 15.2 %all-to-all-start = ((f32[8,16,1536]{2,1,0:T(8,128)}), f32[8,16,1536]{2,1,0:T(8,128)S(1)}, u32[]{:S(2)}, u32[]{:S(2)}) async-start(f32[8,16,1536]{2,1,0:T(8,128)} %get-tuple-element.23), calls=%async_computation | async-start | bytes 1572864 | tf_op jit(solution)/shard_map/all_to_all | solution.py:324
